TPU v7x, 32 devices: a whole 2x2x4 slice. The times are simulated.
32 devices in a mesh: pod: 2 (over x), data: 4 (over z), tensor: 4 (over y, core).
Axes of the slice: x: 2, y: 2, z: 4, core: 2. Of those that a mesh axis runs over, the one named last changes fastest.
Arguments:
- token_ids: int32 [4096], P(('pod', 'data')), parts along dimension 0
- embed_table: bfloat16 [32000, 2048], P('tensor')
- norm_gain: bfloat16 [2048], replicated
- w_in: bfloat16 [2048, 5632], P(None, 'tensor')
- w_out: bfloat16 [5632, 2048], P('tensor')
- d_out: bfloat16 [4096, 2048], P(('pod', 'data', 'tensor')), parts along dimension 0
Outputs:
- output 1: bfloat16 [4096, 2048], P(('pod', 'data', 'tensor')), parts along dimension 0
- output 2: float32 [64000, 2048], P(('pod', 'tensor')), parts along dimension 0
- output 3: float32 [4096, 5632], P('pod', 'tensor'), parts along dimension 0
- output 4: float32 [11264, 2048], P(('pod', 'tensor')), parts along dimension 0
There are 2 independent parts. A program takes and returns all parts, laid end to end along the dimension named above; an argument that names none is the same for every part.
All inputs are finite; a program needn't handle non-finite values.
Results may differ from a plain program's by a relative error of at most 0.00496674.
Values are sent between devices in bfloat16 or wider.
A program may use at most 1 GiB of HBM per device.

v0:
```python
import functools

import jax
import jax.numpy as jnp
from jax import lax
from jax.experimental import pallas as pl
from jax.experimental.pallas import tpu as pltpu
from jax.sharding import PartitionSpec as P


NORM_EPS = 1e-6
GELU_A = 0.7978845608028654
GELU_B = 0.044715
MESH = pl.DeviceIdType.MESH
NT = (((1,), (1,)), ((), ()))
TN = (((0,), (0,)), ((), ()))
F32, BF16, I32 = jnp.float32, jnp.bfloat16, jnp.int32
LANES = 128
XQ = 4
PQ = 4

R_IDS, R_DZ, R_DY, R_DC, R_NZ, R_NC, R_XZ, R_XY, R_XC = 0, 4, 8, 12, 16, 24, 28, 36, 44
R_XM, R_X, R_NO, R_PC, R_PY, N_R = 48, 52, 56, 60, 68, 72
S_IDS, S_DZ, S_DY, S_DC, S_NZ, S_NC, S_XZ, S_XY, S_XC = 0, 3, 8, 12, 16, 26, 30, 40, 48
S_XM, S_X, S_NO, S_PC, S_PY, N_S = 52, 56, 60, 64, 72, 76
L_W1, L_W2, L_XM, L_DX, L_YS, L_YB, L_DW, L_DO, L_K, N_L = 0, 1, 2, 3, 4, 5, 6, 8, 9, 13


def loop(lo, hi, body):
    def one(j, carry):
        body(j)
        return carry

    lax.fori_loop(lo, hi, one, 0)


def tiles(total, step, body):
    full = total // step
    loop(0, full, lambda j: body(pl.multiple_of(j * step, step), step))
    if total % step:
        body(full * step, total % step)


def rows_loop(total, body):
    loop(0, total // 16, lambda j: body(pl.multiple_of(j * 16, 16)))


def sort_keys(ids, keys, place, ordered, first, shard_rows, tall, rank0):
    reps, per, _ = ids.shape
    count = reps * per * LANES
    t = per * LANES // 4
    shift = t.bit_length() - 1
    lines = reps * per
    lane = lax.broadcasted_iota(I32, (per, LANES), 1)
    spot = lax.broadcasted_iota(I32, (per, LANES), 0) * LANES + lane
    block = jnp.right_shift(spot, shift)
    kept = (block & 1) * (2 * t) + jnp.right_shift(block, 1) * t + (spot & (t - 1))
    for k in range(reps):
        row = ids[k] - rank0
        row = jnp.where((row >= 0) & (row < shard_rows), row, shard_rows)
        keys[k * per : (k + 1) * per, :] = (row * count + (k * per * LANES + kept)).astype(F32)
    place[...] = jnp.zeros_like(place)
    ordered[...] = jnp.zeros_like(ordered)
    up = lax.broadcasted_iota(I32, (LANES, LANES), 0)
    over = lax.broadcasted_iota(I32, (LANES, LANES), 1)
    same = up == over
    overf = over.astype(F32)

    def column(ref, b):
        return jnp.sum(jnp.where(same, jnp.broadcast_to(ref[pl.ds(b, 1), :], (LANES, LANES)), 0.0), axis=1, keepdims=True)

    def count_below(b):
        col = column(keys, b)

        def one(a):
            at = pl.ds(a, 1)
            place[at, :] += jnp.sum(jnp.where(col < keys[at, :], 1.0, 0.0), axis=0, keepdims=True)

        loop(0, lines, one)

    loop(0, lines, count_below)

    def put(b):
        col, spot_of = column(keys, b), column(place, b)

        def one(a):
            want = overf + (a * LANES).astype(F32)
            ordered[pl.ds(a, 1), :] += jnp.sum(jnp.where(spot_of == want, col, 0.0), axis=0, keepdims=True)

        loop(0, lines, one)
        edge = overf * float(tall * count)
        first[...] += jnp.sum(jnp.where(col < edge, 1.0, 0.0), axis=0, keepdims=True)

    first[...] = jnp.zeros_like(first)
    loop(0, lines, put)


def group_kernel(shard_rows, tall, ids_ref, xm_hbm, w1_hbm, w2_hbm, g_ref, do_hbm,
                 base_o, ysum_o, ord_o, first_o, dx_o, far_o, dw1_o, dw2_o, nk_o, dk_o, hk_o, duk_o,
                 w1, w2, n, d, xm, xc, xy, hs, dus, pd, pf, rd, rf, yd, yb, dxo, idl, keys, place, ordered, first,
                 lsem, ssem, rsem):
    t, m = do_hbm.shape
    f = w1_hbm.shape[1]
    tq, mq = 2 * t // XQ, m // PQ
    z = lax.axis_index("data")
    r = lax.axis_index("tensor")
    y, c = lax.div(r, 2), lax.rem(r, 2)
    partner = {"tensor": 2 * y + 1 - c}
    across = {"tensor": 2 * (1 - y) + c}
    half = lax.div(z, 2)
    inner = z + half * (3 - 2 * z)
    order = [b + half * (3 - 2 * b) for b in (1 - inner, 2, 3)]
    middle, end = inner == 1, inner == 0

    def row(zz, cc, yy=0):
        return pl.multiple_of(zz * (4 * t) + cc * (2 * t) + yy * t, t)

    def blk(ref, zz, cc, yy):
        return ref.at[pl.ds(row(zz, cc, yy), t)]

    def duo(ref, zz, cc):
        return ref.at[pl.ds(row(zz, cc), 2 * t)]

    def remote(src, dst, s, q, dev):
        return pltpu.make_async_remote_copy(
            src_ref=src, dst_ref=dst, send_sem=ssem.at[s], recv_sem=rsem.at[q], device_id=dev, device_id_type=MESH
        )

    def local(src, dst, i):
        return pltpu.make_async_copy(src, dst, lsem.at[i])

    def arrived(ref, q):
        remote(ref, ref, 0, q, partner).wait_recv()

    def start(cp):
        cp.start()

    def sent(cp):
        cp.wait_send()

    def along(src, dst, s, q, act):
        for i, hop in enumerate((1, -1)):
            to = z + hop

            @pl.when((to >= 0) & (to <= 3))
            def _():
                act(remote(src, dst, s + i, q + z, {"data": to}))

    def pass_on(k, ref, s, q, act):
        src, dst = ref if isinstance(ref, tuple) else (ref, ref)
        act(remote(src, dst, s + 2 + k, q + order[k], {"data": order[1] if k == 0 else order[0]}))

    barrier = pltpu.get_barrier_semaphore()
    pl.semaphore_signal(barrier, inc=1, device_id=partner, device_id_type=MESH)
    pl.semaphore_signal(barrier, inc=1, device_id=across, device_id_type=MESH)
    for k in range(3):
        pl.semaphore_signal(barrier, inc=1, device_id={"data": order[k]}, device_id_type=MESH)

    own_d = blk(d, z, c, y)
    local(do_hbm, own_d, L_DO).start()
    local(xm_hbm, xm, L_XM).start()
    local(w1_hbm, w1, L_W1).start()
    local(w2_hbm, w2, L_W2).start()
    pl.semaphore_wait(barrier, 5)

    def piece(q):
        return pl.ds(q * tq, tq)

    for k in range(3):
        remote(ids_ref, idl.at[z], S_IDS + k, R_IDS + z, {"data": order[k]}).start()
    idl[z] = ids_ref[...]

    local(do_hbm, own_d, L_DO).wait()
    along(own_d, own_d, S_DZ, R_DZ, start)
    local(xm_hbm, xm, L_XM).wait()

    def xm_part(q):
        return remote(xm.at[pl.ds(row(0, 1 - c) + q * tq, tq)], xc.at[piece(q)], S_XM + q, R_XM + q, partner)

    def x_part(q):
        return remote(xc.at[piece(q)], xy.at[piece(q)], S_X + q, R_X + q, across)

    def d_got(k):
        arrived(blk(d, order[k], c, y), R_DZ + order[k])

    def d_on(k):
        pass_on(k, blk(d, order[k], c, y), S_DZ, R_DZ, start)

    def d_across(zz, act):
        act(remote(blk(d, zz, c, y), blk(d, zz, c, y), S_DY + zz, R_DY + zz, across))

    def d_pair(zz, act):
        act(remote(duo(d, zz, c), duo(d, zz, c), S_DC + zz, R_DC + zz, partner))

    for q in range(XQ):
        xm_part(q).start()
    for q in range(XQ):
        arrived(xc.at[piece(q)], R_XM + q)

        def join(i, q=q):
            at = pl.ds(q * tq + i, 16)
            xc[at, :] += xm[pl.ds(row(0, c) + q * tq + i, 16), :]

        rows_loop(tq, join)
        x_part(q).start()
    d_across(z, start)

    d_got(0)

    @pl.when(middle)
    def _():
        d_on(0)
        d_got(1)
        d_on(1)

    gain = jnp.concatenate([g_ref[pl.ds(i, 1), :] for i in range(m // LANES)], axis=1).astype(F32)

    def n_own(q, act):
        at = n.at[pl.ds(row(z, c) + q * tq, tq)]
        act(remote(at, at, S_NO + q, R_NO + q, partner))

    def n_along(b, act):
        ref = blk(n, z, c, b)
        along(ref, ref, S_NZ + 5 * b, R_NZ + 4 * b, act)

    for q in range(XQ):
        arrived(xy.at[piece(q)], R_X + q)
        x_part(q).wait_send()

        def norm(i, q=q):
            at = pl.ds(q * tq + i, 16)
            x16 = xc[at, :] + xy[at, :]
            xc[at, :] = x16
            x = x16.astype(F32)
            s = lax.rsqrt(jnp.mean(x * x, axis=-1, keepdims=True) + NORM_EPS)
            n[pl.ds(row(z, c) + q * tq + i, 16), :] = ((x * s) * gain).astype(BF16)

        rows_loop(tq, norm)
        n_own(q, start)
        if q == XQ // 2 - 1:
            n_along(0, start)

            @pl.when(middle)
            def _():
                d_got(2)
                d_on(2)

        if q == XQ - 1:
            n_along(1, start)
    d_across(order[0], start)

    def hidden(zz, slopes):
        at = pl.ds(row(zz, 0), 4 * t)

        def body(off, w):
            to = pl.ds(off, w)
            u = jnp.dot(n[at, :], w1[:, to], preferred_element_type=F32).astype(BF16).astype(F32)
            uu = u * u
            th = jnp.tanh(GELU_A * (u + GELU_B * (uu * u)))
            cdf = 0.5 * (1.0 + th)
            hs[at, to] = (u * cdf).astype(BF16)
            slopes[:, to] = cdf + (0.5 * GELU_A) * u * (1.0 - th * th) * (1.0 + (3.0 * GELU_B) * uu)

        tiles(f, 256, body)

    def grad_hidden(zz, slopes):
        at = pl.ds(row(zz, 0), 4 * t)

        def body(off, w):
            to = pl.ds(off, w)
            dh = lax.dot_general(d[at, :], w2[to, :], NT, preferred_element_type=F32)
            dus[at, to] = (dh * slopes[:, to]).astype(BF16)

        tiles(f, 256, body)

    for q in range(XQ):
        arrived(n.at[pl.ds(row(z, 1 - c) + q * tq, tq)], R_NO + q)
    local(w1_hbm, w1, L_W1).wait()
    hidden(z, pf)
    arrived(blk(d, z, c, 1 - y), R_DY + z)
    d_pair(z, start)
    arrived(duo(d, z, 1 - c), R_DC + z)
    local(w2_hbm, w2, L_W2).wait()
    grad_hidden(z, pf)

    own_rows = pl.ds(row(z, 0), 4 * t)
    far = pl.multiple_of((1 - y) * t, t)

    def cols(q):
        return pl.ds(pl.multiple_of(q * mq, mq), mq)

    def part_pair(src, dst, i, q):
        return remote(src.at[pl.ds(row(0, 1 - c), 2 * t), cols(q)], dst.at[:, cols(q)], S_PC + PQ * i + q, R_PC + PQ * i + q, partner)

    def part_across(q):
        return remote(rd.at[pl.ds(far, t), cols(q)], yd.at[:, cols(q)], S_PY + q, R_PY + q, across)

    def sum_part(part, got, i, q):
        arrived(got.at[:, cols(q)], R_PC + PQ * i + q)

        def add(k):
            got[pl.ds(far + k, 16), cols(q)] += part[pl.ds(row(0, c, 1 - y) + k, 16), cols(q)]

        rows_loop(t, add)

    def dn_part(q):
        pd[:, cols(q)] = lax.dot_general(dus[own_rows, :], w1[cols(q), :], NT, preferred_element_type=F32)
        part_pair(pd, rd, 0, q).start()

    def y_part(q):
        pf[:, cols(q)] = jnp.dot(hs[own_rows, :], w2[:, cols(q)], preferred_element_type=F32)
        part_pair(pf, rf, 1, q).start()

    def dn_out(q):
        sum_part(pd, rd, 0, q)
        part_across(q).start()

    loop(0, PQ, dn_part)
    loop(0, PQ, dn_out)
    loop(0, PQ, y_part)

    @pl.when(end)
    def _():
        d_got(1)

    d_across(order[1], start)

    loop(0, PQ, lambda q: sum_part(pf, rf, 1, q))
    y_send = local(rf.at[pl.ds(far, t)], ysum_o, L_YS)
    y_send.start()

    def base(i):
        own = pl.ds(y * t + i, 16)
        yb[pl.ds(i, 16), :] = xc[own, :].astype(F32) + (pf[pl.ds(row(0, c, y) + i, 16), :] + rf[own, :])

    rows_loop(t, base)
    y_keep = local(yb, base_o, L_YB)
    y_keep.start()
    for q in range(PQ):
        part_pair(pf, rf, 1, q).wait_send()

    def n_got(k):
        for b in range(2):
            arrived(blk(n, order[k], c, b), R_NZ + 4 * b + order[k])

    def n_on(k):
        for b in range(2):
            pass_on(k, blk(n, order[k], c, b), S_NZ + 5 * b, R_NZ + 4 * b, start)

    def n_pair(zz, act):
        act(remote(duo(n, zz, c), duo(n, zz, c), S_NC + zz, R_NC + zz, partner))

    n_got(0)
    n_pair(order[0], start)

    @pl.when(middle)
    def _():
        n_on(0)
        n_got(1)
        n_on(1)
        n_pair(order[1], start)

    def unit(k, slopes):
        zz = order[k]
        arrived(blk(d, zz, c, 1 - y), R_DY + zz)
        d_pair(zz, start)
        arrived(duo(n, zz, 1 - c), R_NC + zz)
        hidden(zz, slopes)
        arrived(duo(d, zz, 1 - c), R_DC + zz)
        grad_hidden(zz, slopes)

    def n_rest(k, on):
        n_got(k)
        if on:
            n_on(k)
        n_pair(order[k], start)

    unit(0, pf)

    for q in range(PQ):
        arrived(yd.at[:, cols(q)], R_PY + q)

    def grad_x(i):
        at, own = pl.ds(i, 16), pl.ds(y * t + i, 16)
        dn = pd[pl.ds(row(0, c, y) + i, 16), :] + rd[own, :] + yd[at, :]
        x = xc[own, :].astype(F32)
        s = lax.rsqrt(jnp.mean(x * x, axis=-1, keepdims=True) + NORM_EPS)
        xh = x * s
        dhat = dn * gain
        dxn = s * (dhat - xh * jnp.mean(dhat * xh, axis=-1, keepdims=True))
        dxo[at, :] = (d[pl.ds(row(z, c, y) + i, 16), :].astype(F32) + dxn).astype(BF16)

    rows_loop(t, grad_x)
    th = t // 2

    def dx_part(zz, yy, h):
        return dx_o.at[pl.ds(pl.multiple_of(row(zz, c, yy) + h * th, th), th)]

    def dx_own(h):
        return dxo.at[pl.ds(h * th, th)]

    def far_part(h):
        return far_o.at[pl.ds(h * th, th)]

    def dx_next(k, h):
        here = dx_part(order[k], y, h)
        return (here, here) if k == 1 else (here if k == 0 else far_part(h), far_part(h))

    def dx_across(zz, src, h, act):
        act(remote(src, dx_part(zz, y, h), S_XY + 4 * h + zz, R_XY + 4 * h + zz, across))

    def dx_along(act):
        for h in range(2):
            along(dx_own(h), dx_part(z, y, h), S_XZ + 5 * h, R_XZ + 4 * h, act)

    def dx_pair(zz, act):
        act(remote(duo(dx_o, zz, c), duo(dx_o, zz, c), S_XC + zz, R_XC + zz, partner))

    def dx_got(k, on):
        zz = order[k]
        for h in range(2):
            arrived(dx_part(zz, y, h) if k < 2 else far_part(h), R_XZ + 4 * h + zz)
            if on:
                pass_on(k, dx_next(k, h), S_XZ + 5 * h, R_XZ + 4 * h, start)
            if k < 2:
                dx_across(zz, dx_part(zz, y, h), h, start)

    def dx_hand(zz):
        for h in range(2):
            arrived(dx_part(zz, 1 - y, h), R_XY + 4 * h + zz)
        dx_pair(zz, start)

    for h in range(2):
        dx_across(z, dx_own(h), h, start)
    local(dxo, blk(dx_o, z, c, y), L_DX).start()

    @pl.when(end)
    def _():
        d_got(2)

    d_across(order[2], start)

    for q in range(PQ):
        part_pair(pd, rd, 0, q).wait_send()

    pl.when(middle)(lambda: n_rest(2, True))
    dx_along(start)
    pl.when(end)(lambda: n_rest(1, False))
    unit(1, pd)

    @pl.when(middle)
    def _():
        dx_got(0, True)
        dx_got(1, True)

    tw = 2 * t
    n1, n2 = m // tw, f // tw
    late_rows = pl.ds(row(order[2], 0), 4 * t)
    early_rows = pl.ds(pl.multiple_of(half * (4 * t), 4 * t), 12 * t)

    def flush(i, buf, dst):
        lines = pl.ds(pl.multiple_of(lax.rem(i, 2) * tw, tw), tw)
        here = buf.at[lines, pl.ds(0, dst.shape[1])]
        return here, local(here, dst.at[pl.ds(pl.multiple_of(i * tw, tw), tw)], L_DW + lax.rem(i, 2))

    def weight_tile(i, lhs, rhs, buf, dst):
        pl.when(i >= 2)(lambda: flush(i - 2, buf, dst)[1].wait())
        here, out = flush(i, buf, dst)
        at = pl.ds(pl.multiple_of(i * tw, tw), tw)
        here[...] = lax.dot_general(lhs[early_rows, at], rhs[early_rows, :], TN, preferred_element_type=F32)
        out.start()

    loop(0, n1, lambda i: weight_tile(i, n, dus, pf, dw1_o))
    for i in (n1 - 2, n1 - 1):
        flush(i, pf, dw1_o)[1].wait()
    pl.when(end)(lambda: n_rest(2, False))
    unit(2, pd)
    kept = [
        local(src.at[late_rows], dst, L_K + i)
        for i, (src, dst) in enumerate(((n, nk_o), (d, dk_o), (hs, hk_o), (dus, duk_o)))
    ]
    for cp in kept:
        cp.start()
    pl.when(end)(lambda: dx_got(0, False))
    pl.when(middle)(lambda: dx_got(2, True))
    loop(0, n2 // 2, lambda i: weight_tile(i, hs, d, pd, dw2_o))
    pl.when(end)(lambda: dx_got(1, False))
    loop(n2 // 2, n2, lambda i: weight_tile(i, hs, d, pd, dw2_o))
    local(dxo, blk(dx_o, z, c, y), L_DX).wait()
    dx_hand(z)
    dx_hand(order[0])

    for k in range(3):
        arrived(idl.at[order[k]], R_IDS + order[k])
    sort_keys(idl, keys, place, ordered, first, shard_rows, tall, r * shard_rows)
    ord_o[...] = ordered[...].astype(I32)
    first_o[...] = first[...].astype(I32)

    for i in (n2 - 2, n2 - 1):
        flush(i, pd, dw2_o)[1].wait()
    if f % tw:
        rest = pd.at[pl.ds(0, f % tw)]
        rest[...] = lax.dot_general(hs[early_rows, n2 * tw :], d[early_rows, :], TN, preferred_element_type=F32)
        last = local(rest, dw2_o.at[pl.ds(n2 * tw, f % tw)], L_DW)
        last.start()
    dx_hand(order[1])
    pl.when(end)(lambda: dx_got(2, False))
    if f % tw:
        last.wait()
    for cp in kept:
        cp.wait()

    y_send.wait()
    y_keep.wait()
    along(own_d, own_d, S_DZ, R_DZ, sent)
    for zz in (z, *order):
        d_across(zz, sent)
        d_pair(zz, sent)
    for k in range(3):
        n_pair(order[k], sent)
        remote(ids_ref, idl.at[z], S_IDS + k, R_IDS + z, {"data": order[k]}).wait_send()
    dx_along(sent)
    for b in range(2):
        n_along(b, sent)
        dx_across(z, dx_own(b), b, sent)
        for k in range(2):
            dx_across(order[k], dx_part(order[k], y, b), b, sent)

    @pl.when(middle)
    def _():
        for k in range(3):
            pass_on(k, blk(d, order[k], c, y), S_DZ, R_DZ, sent)
            for b in range(2):
                pass_on(k, dx_next(k, b), S_XZ + 5 * b, R_XZ + 4 * b, sent)
                pass_on(k, blk(n, order[k], c, b), S_NZ + 5 * b, R_NZ + 4 * b, sent)

    for q in range(XQ):
        xm_part(q).wait_send()
        n_own(q, sent)
    for q in range(PQ):
        part_across(q).wait_send()
    for zz in (z, *order[:2]):
        arrived(duo(dx_o, zz, 1 - c), R_XC + zz)
        dx_pair(zz, sent)


def run_group(ids, xm, w1, w2, gain, d_out, shard_rows, tall):
    t, m = d_out.shape
    f = w1.shape[1]
    lines = 4 * ids.shape[0]
    any_, vmem = pl.BlockSpec(memory_space=pl.ANY), pl.BlockSpec(memory_space=pltpu.VMEM)
    V = pltpu.VMEM
    sds = jax.ShapeDtypeStruct
    dots = 2 * 4 * t * m * f
    return pl.pallas_call(
        functools.partial(group_kernel, shard_rows, tall),
        out_shape=(
            sds((t, m), F32), sds((t, m), F32), sds((lines, LANES), I32), sds((1, LANES), I32), sds((16 * t, m), BF16),
            sds((t, m), BF16), sds((m, f), F32), sds((f, m), F32),
            sds((4 * t, m), BF16), sds((4 * t, m), BF16), sds((4 * t, f), BF16), sds((4 * t, f), BF16),
        ),
        in_specs=[vmem, any_, any_, any_, vmem, any_],
        out_specs=(any_, any_, vmem, vmem, *[any_] * 8),
        scratch_shapes=[
            V((m, f), BF16), V((f, m), BF16), V((16 * t, m), BF16), V((16 * t, m), BF16),
            V((4 * t, m), BF16), V((2 * t, m), BF16), V((2 * t, m), BF16),
            V((16 * t, f), BF16), V((16 * t, f), BF16),
            V((4 * t, m), F32), V((4 * t, m), F32), V((2 * t, m), F32), V((2 * t, m), F32),
            V((t, m), F32), V((t, m), F32),
            V((t, m), BF16), V((4, *ids.shape), I32),
            V((lines, LANES), F32), V((lines, LANES), F32), V((lines, LANES), F32), V((1, LANES), F32),
            pltpu.SemaphoreType.DMA((N_L,)), pltpu.SemaphoreType.DMA((N_S,)), pltpu.SemaphoreType.DMA((N_R,)),
        ],
        compiler_params=pltpu.CompilerParams(collective_id=0, has_side_effects=True, vmem_limit_bytes=67043328),
        cost_estimate=pl.CostEstimate(flops=18 * dots, bytes_accessed=64 * 16 * t * m, transcendentals=16 * t * f),
        name="group_step",
    )(ids, xm, w1, w2, gain, d_out)


def lookup_kernel(shard_rows, ids_smem, ids_vmem, table, out_hbm, got, rows, sem, out_sem):
    total, m = out_hbm.shape
    t = total // 4
    per = 32
    chunks = total // per
    r = lax.axis_index("tensor")
    spread = (1 << (shard_rows.bit_length() - 1)) - 1

    def fetch(k):
        def some(j, carry):
            for u in range(8):
                p = k * per + j * 8 + u
                row = ids_smem[jnp.right_shift(p, 7), p & (LANES - 1)]
                near = row - r * shard_rows
                near = jnp.where((near >= 0) & (near < shard_rows), near, row & spread)
                pltpu.make_async_copy(table.at[jnp.right_shift(near, 3)], got.at[p], sem.at[k]).start()
            return carry

        lax.fori_loop(0, per // 8, some, 0)

    loop(0, chunks, fetch)
    spot = lax.broadcasted_iota(I32, (per, 8 * per), 1)
    token = lax.broadcasted_iota(I32, (per, 8 * per), 0)
    same = lax.broadcasted_iota(I32, (LANES, LANES), 0) == lax.broadcasted_iota(I32, (LANES, LANES), 1)

    def line(b):
        ids = ids_vmem[pl.ds(b, 1), :].astype(F32)
        col = jnp.sum(jnp.where(same, jnp.broadcast_to(ids, (LANES, LANES)), 0.0), axis=1, keepdims=True).astype(I32)
        row = col - r * shard_rows
        row = jnp.where((row >= 0) & (row < shard_rows), row & 7, -8 * per)
        for j in range(LANES // per):
            k = b * (LANES // per) + j
            at = pl.ds(pl.multiple_of(k * per, per), per)
            pltpu.make_async_copy(got.at[at], got.at[at], sem.at[k]).wait()
            want = row[j * per : (j + 1) * per] + 8 * token
            chosen = jnp.where(want == spot, 1.0, 0.0).astype(BF16)
            picked = jnp.dot(chosen, got[at].reshape(8 * per, m), preferred_element_type=F32)
            p = k * per
            nat = lax.div(p, t)
            to = pl.multiple_of(lax.rem(nat, 2) * (2 * t) + lax.div(nat, 2) * t + lax.rem(p, t), per)
            rows[pl.ds(to, per), :] = picked.astype(BF16)
            pltpu.make_async_copy(rows.at[pl.ds(to, per)], out_hbm.at[pl.ds(to, per)], out_sem).start()

    loop(0, total // LANES, line)
    pltpu.make_async_copy(rows, out_hbm, out_sem).wait()


def look_up(ids, table):
    shard_rows, m = table.shape
    total = ids.size
    any_ = pl.BlockSpec(memory_space=pl.ANY)
    return pl.pallas_call(
        functools.partial(lookup_kernel, shard_rows),
        out_shape=jax.ShapeDtypeStruct((total, m), BF16),
        in_specs=[pl.BlockSpec(memory_space=pltpu.SMEM), pl.BlockSpec(memory_space=pltpu.VMEM), any_],
        out_specs=any_,
        scratch_shapes=[
            pltpu.VMEM((total, 8, m), BF16), pltpu.VMEM((total, m), BF16),
            pltpu.SemaphoreType.DMA((total // 32,)), pltpu.SemaphoreType.DMA,
        ],
        compiler_params=pltpu.CompilerParams(vmem_limit_bytes=60 << 20),
        cost_estimate=pl.CostEstimate(flops=16 * total * m, bytes_accessed=20 * total * m, transcendentals=0),
        name="look_up",
    )(ids, ids, table.reshape(shard_rows // 8, 8, m))


RING = 6


def weights_kernel(p1, p2, nk_in, dk_in, hk_in, duk_in, o1, o2, b1, b2, nk, dk, hk, duk, in_sem, out_sem, k_sem):
    m, f = b1.shape
    tw = nk.shape[0] // 2
    ins = [pltpu.make_async_copy(a, b, k_sem.at[i]) for i, (a, b) in enumerate(((nk_in, nk), (duk_in, duk), (hk_in, hk), (dk_in, dk)))]
    for cp in ins[:2]:
        cp.start()

    def part(src, buf, dst, first, i, rows=tw):
        at = pl.ds(pl.multiple_of(i * tw, 8), rows)
        fetch = pltpu.make_async_copy(src.at[at], buf.at[at], in_sem.at[first + i])
        return fetch, pltpu.make_async_copy(buf.at[at], dst.at[at], out_sem)

    def fetch_all(src, buf, dst, first):
        loop(0, src.shape[0] // tw, lambda i: part(src, buf, dst, first, i)[0].start())

    n1, n2 = m // tw, f // tw
    fetch_all(p1, b1, o1, 0)
    for cp in ins[2:]:
        cp.start()
    fetch_all(p2, b2, o2, n1)
    rest = [part(p2, b2, o2, n1, n2, f % tw)] if f % tw else []
    for come, _ in rest:
        come.start()

    def add(src, buf, dst, first, lhs, rhs, i, rows=tw):
        come, go = part(src, buf, dst, first, i, rows)
        come.wait()
        cols = pl.ds(pl.multiple_of(i * tw, tw), rows)
        buf[cols, :] += lax.dot_general(lhs[:, cols], rhs[...], TN, preferred_element_type=F32)
        go.start()

    for cp in ins[:2]:
        cp.wait()
    loop(0, n1, lambda i: add(p1, b1, o1, 0, nk, duk, i))
    for cp in ins[2:]:
        cp.wait()
    loop(0, n2, lambda i: add(p2, b2, o2, n1, hk, dk, i))
    if rest:
        add(p2, b2, o2, n1, hk, dk, n2, f % tw)
    pltpu.make_async_copy(b1, o1, out_sem).wait()
    pltpu.make_async_copy(b2, o2, out_sem).wait()


def finish_weights(p1, p2, nk, dk, hk, duk):
    any_ = pl.BlockSpec(memory_space=pl.ANY)
    V, S = pltpu.VMEM, pltpu.SemaphoreType.DMA
    arrays = (p1, p2, nk, dk, hk, duk)
    return pl.pallas_call(
        weights_kernel,
        out_shape=(jax.ShapeDtypeStruct(p1.shape, F32), jax.ShapeDtypeStruct(p2.shape, F32)),
        in_specs=[any_] * 6,
        out_specs=[any_] * 2,
        scratch_shapes=[*[V(a.shape, a.dtype) for a in arrays], S((32,)), S, S((4,))],
        compiler_params=pltpu.CompilerParams(vmem_limit_bytes=60 << 20),
        cost_estimate=pl.CostEstimate(flops=8000 * p1.size, bytes_accessed=20 * p1.size, transcendentals=0),
        name="finish_weights",
    )(*arrays)


def table_kernel(tall, key_ref, first_ref, dx_in, far_own, far_across, far_partner, far_both, out_hbm, dxb, dxf, ring, dx_sem, t_sem):
    count, _ = dxb.shape
    t = count // 16
    shift = count.bit_length() - 1
    steps = out_hbm.shape[0] // tall
    z, r = lax.axis_index("data"), lax.axis_index("tensor")
    y, c = lax.div(r, 2), lax.rem(r, 2)
    late = lax.div(z, 2)

    def near(k):
        at = pl.ds(pl.multiple_of(late * (4 * t) + k * (2 * t), t), 2 * t)
        return at, pltpu.make_async_copy(dx_in.at[at], dxb.at[at], dx_sem.at[k])

    def far(k, src, cc, yy):
        at = pl.ds(pl.multiple_of((1 - late) * (12 * t) + cc * (2 * t) + yy * t, t), t)
        return at, pltpu.make_async_copy(src, dxb.at[at], dx_sem.at[6 + k])

    fars = ((far_own, c, y), (far_across, c, 1 - y), (far_partner, 1 - c, y), (far_both, 1 - c, 1 - y))
    loop(0, 6, lambda k: near(k)[1].start())
    for k, what in enumerate(fars):
        far(k, *what)[1].start()

    def widen_piece(at, cp):
        cp.wait()

        def widen(i):
            rows = pl.ds(pl.multiple_of(at.start + i, 16), 16)
            dxf[rows, :] = dxb[rows, :].astype(F32)

        rows_loop(at.size, widen)

    loop(0, 6, lambda k: widen_piece(*near(k)))
    for k, what in enumerate(fars):
        widen_piece(*far(k, *what))

    def tile_out(i):
        slot = lax.rem(i, RING)
        return pltpu.make_async_copy(ring.at[slot], out_hbm.at[pl.ds(pl.multiple_of(i * tall, 8), tall)], t_sem.at[slot])

    def tile(i):
        slot = lax.rem(i, RING)
        here = ring.at[slot]
        pl.when(i >= RING)(lambda: tile_out(i - RING).wait())
        here[...] = jnp.zeros_like(here)

        def add(j, key):
            ahead = key_ref[jnp.minimum(j + 1, count - 1)]
            to = pl.ds(jnp.right_shift(key, shift) - i * tall, 1)
            here[to, :] += dxf[pl.ds(key & (count - 1), 1), :]
            return ahead

        low = first_ref[i]
        lax.fori_loop(low, first_ref[i + 1], add, key_ref[jnp.minimum(low, count - 1)])
        tile_out(i).start()

    loop(0, steps, tile)
    loop(steps - RING, steps, lambda i: tile_out(i).wait())


def table_grad(ordered, first, dx_all, fars, shard_rows, tall):
    count, m = dx_all.shape
    any_ = pl.BlockSpec(memory_space=pl.ANY)
    V, S = pltpu.VMEM, pltpu.SemaphoreType.DMA
    return pl.pallas_call(
        functools.partial(table_kernel, tall),
        out_shape=jax.ShapeDtypeStruct((shard_rows, m), F32),
        grid_spec=pltpu.PrefetchScalarGridSpec(
            num_scalar_prefetch=2,
            grid=(1,),
            in_specs=[any_] * 5,
            out_specs=any_,
            scratch_shapes=[
                V((count, m), BF16), V((count, m), F32), V((RING, tall, m), F32), S((10,)), S((RING,)),
            ],
        ),
        compiler_params=pltpu.CompilerParams(vmem_limit_bytes=60 << 20),
        cost_estimate=pl.CostEstimate(flops=16000 * shard_rows * m // 10, bytes_accessed=4 * shard_rows * m, transcendentals=0),
        name="table_grad",
    )(ordered, first, dx_all, *fars)


def solution(mesh):
    tok_spec = P(("pod", "data", "tensor"), None)

    over_y, over_core = [(0, 2), (1, 3), (2, 0), (3, 1)], [(0, 1), (1, 0), (2, 3), (3, 2)]

    def per_device(token_ids, embed_table, norm_gain, w_in, w_out, d_out):
        shard_rows = embed_table.shape[0]
        tall = next(k for k in (160, 8) if shard_rows % k == 0)
        ids = token_ids.reshape(-1, LANES)
        masked = look_up(ids, embed_table)
        gain = norm_gain.reshape(-1, LANES)
        base, ysum, ordered, first, dx_all, far, *weights = run_group(
            ids, masked, w_in, w_out, gain, d_out, shard_rows, tall
        )
        far_x = lax.ppermute(far, "tensor", over_y)
        far_p = lax.ppermute(far, "tensor", over_core)
        other = lax.ppermute(ysum, "tensor", over_y)
        grad_w_in, grad_w_out = finish_weights(*weights)
        far_b = lax.ppermute(far_x, "tensor", over_core)
        fars = (far, far_x, far_p, far_b)
        grad_table = table_grad(ordered.reshape(-1), first.reshape(-1), dx_all, fars, shard_rows, tall)
        return (base + other).astype(BF16), grad_table, grad_w_in, grad_w_out

    return jax.shard_map(
        per_device,
        mesh=mesh,
        in_specs=(P(("pod", "data")), P("tensor", None), P(None), P(None, "tensor"), P("tensor", None), tok_spec),
        out_specs=(tok_spec, P(("pod", "tensor"), None), P("pod", "tensor"), P(("pod", "tensor"), None)),
        check_vma=False,
    )
```

profile of v0, /device:TPU:0, one launch (start us, length us, event | category | flops | bytes accessed | tf_op | source)
XLA Modules:
  0.0 237.0 jit_solution(1242705583718779429)
XLA Ops:
  0.6 9.8 %look_up.1.xm_hbm = bf16[512,2048]{1,0:T(8,128)(2,1)} custom-call(s32[4,128]{1,0:T(4,128)} %bitcast.6, s32[4,128]{1,0:T(4,128)} %bitcast.7, bf16[1000,8,2048]{2,1,0:T(8,128)(2,1)} %bitcast.5), custom_call_target="tpu_custom_call" | custom-call | flops 16777216 | bytes 20971520 | tf_op jit(solution)/shard_map/look_up/pallas_call | solution.py:631
  10.5 162.3 %group_step.1 = (f32[128,2048]{1,0:T(8,128)}, f32[128,2048]{1,0:T(8,128)}, s32[16,128]{1,0:T(8,128)}, s32[1,128]{1,0:T(1,128)}, bf16[2048,2048]{1,0:T(8,128)(2,1...) custom-call(s32[4,128]{1,0:T(4,128)} %bitcast.8, ...), custom_call_target="tpu_custom_call" | custom-call | flops 53150220288 | bytes 268435456 | tf_op jit(solution)/shard_map/group_step/pallas_call | solution.py:555
  172.8 0.4 collective-permute-start.1
  173.1 0.2 collective-permute-start.2
  173.3 1.7 collective-permute-start
  175.0 12.9 %collective-permute-done.1.far_across = bf16[128,2048]{1,0:T(8,128)(2,1)S(1)} collective-permute-done((bf16[128,2048]{1,0:T(8,128)(2,1)}, bf16[128,2048]{1,0:T(8,128)(2,1)S(1)}, u32[]{:S(2)}, u32[]{:S(2)}) %collective-permute-start.1) | collective-permute-done | bytes 524320 | tf_op jit(solution)/shard_map/ppermute | solution.py:803
  187.8 0.0 copy-start.1
  187.8 0.0 collective-permute-start.3
  187.8 0.0 copy-start
  187.8 17.9 %finish_weights.1 = (f32[2048,1408]{1,0:T(8,128)}, f32[1408,2048]{1,0:T(8,128)}) custom-call(f32[2048,1408]{1,0:T(8,128)} %get-tuple-element.24.p1, f32[1408,2048]{1,0:T(8,128)} %get-tuple-element.25.p2, bf16[512,2048]{1,0:T(8,128)(2,1)} %get-tuple-element.26.nk_in, bf16[512,2048]{1,0:T(8,128)(2,1)} %get-tuple-element.27.dk_in, ...), custom_call_target="tpu_custom_call" | custom-call | flops 23068672000 | bytes 57671680 | tf_op jit(solution)/shard_map/finish_weights/pallas_call | solution.py:696
  205.8 0.0 copy-done.1
  205.8 4.0 %collective-permute-done = f32[128,2048]{1,0:T(8,128)S(1)} collective-permute-done((f32[128,2048]{1,0:T(8,128)}, f32[128,2048]{1,0:T(8,128)S(1)}, u32[]{:S(2)}, u32[]{:S(2)}) %collective-permute-start) | collective-permute-done | bytes 1048608 | tf_op jit(solution)/shard_map/ppermute | solution.py:805
  209.7 0.0 copy-done
  209.7 0.9 add_convert_fusion
  210.6 0.0 collective-permute-done.2.far_partner
  210.6 0.0 copy-start.2
  210.6 0.0 collective-permute-done.3.far_both
  210.6 0.0 copy-start.3
  210.7 0.8 copy-done.2
  211.4 0.2 copy-done.3
  211.6 25.3 %table_grad.1 = f32[8000,2048]{1,0:T(8,128)} custom-call(s32[2048]{0:T(1024)} %bitcast.10, s32[128]{0:T(128)} %bitcast.11, bf16[2048,2048]{1,0:T(8,128)(2,1)} %get-tuple-element.22.dx_in, bf16[128,2048]{1,0:T(8,128)(2,1)} %get-tuple-element.23.far_own, bf16[128,2048]{1,0:T(8,128)(2,1)} %copy-done.1, bf16[128,2048]{1,0:T(8,128)(2,1)} %copy-done.2, ...), custom_call_target="tpu_custom_call" | custom-call | flops 26214400000 | bytes 65536000 | tf_op jit(solution)/shard_map/table_grad/pallas_call | solution.py:771
Async XLA Ops:
  172.8 15.1 %collective-permute-start.1 = (bf16[128,2048]{1,0:T(8,128)(2,1)}, bf16[128,2048]{1,0:T(8,128)(2,1)S(1)}, u32[]{:S(2)}, u32[]{:S(2)}) collective-permute-start(bf16[128,2048]{1,0:T(8,128)(2,1)} %get-tuple-element.23.far_own), channel_id=1, source_target_pairs={{0,2},{1,3},{2,0},{3,1},{4,6},{5,7},{6,4},{7,5},{8,10},{9,11},{10,... | collective-permute-start | bytes 1572872 | tf_op jit(solution)/shard_map/ppermute | solution.py:803
  173.1 37.5 %collective-permute-start.2 = (bf16[128,2048]{1,0:T(8,128)(2,1)}, bf16[128,2048]{1,0:T(8,128)(2,1)S(1)}, u32[]{:S(2)}, u32[]{:S(2)}) collective-permute-start(bf16[128,2048]{1,0:T(8,128)(2,1)} %get-tuple-element.23.far_own), channel_id=1, source_target_pairs={{0,1},{1,0},{2,3},{3,2},{4,5},{5,4},{6,7},{7,6},{8,9},{9,8},{10,11... | collective-permute-start | bytes 1572872 | tf_op jit(solution)/shard_map/ppermute | solution.py:804
  173.3 36.4 %collective-permute-start = (f32[128,2048]{1,0:T(8,128)}, f32[128,2048]{1,0:T(8,128)S(1)}, u32[]{:S(2)}, u32[]{:S(2)}) collective-permute-start(f32[128,2048]{1,0:T(8,128)} %get-tuple-element.19), channel_id=1, source_target_pairs={{0,2},{1,3},{2,0},{3,1},{4,6},{5,7},{6,4},{7,5},{8,10},{9,11},{10,... | collective-permute-start | bytes 3145736 | tf_op jit(solution)/shard_map/ppermute | solution.py:805
  187.8 17.9 %copy-start.1 = (bf16[128,2048]{1,0:T(8,128)(2,1)}, bf16[128,2048]{1,0:T(8,128)(2,1)S(1)}, u32[]{:S(2)}) copy-start(bf16[128,2048]{1,0:T(8,128)(2,1)S(1)} %collective-permute-done.1.far_across) | copy-start | bytes 1572868
  187.8 22.8 %collective-permute-start.3 = (bf16[128,2048]{1,0:T(8,128)(2,1)S(1)}, bf16[128,2048]{1,0:T(8,128)(2,1)S(1)}, u32[]{:S(2)}, u32[]{:S(2)}) collective-permute-start(bf16[128,2048]{1,0:T(8,128)(2,1)S(1)} %collective-permute-done.1.far_across), channel_id=1, source_target_pairs={{0,1},{1,0},{2,3},{3,2},{4,5},{5,4},{6,7},{7,6},{8,9},{9,8},{10,11... | collective-permute-start | bytes 1572872 | tf_op jit(solution)/shard_map/ppermute | solution.py:807
  187.8 21.9 %copy-start = (f32[128,2048]{1,0:T(8,128)S(1)}, f32[128,2048]{1,0:T(8,128)}, u32[]{:S(2)}) copy-start(f32[128,2048]{1,0:T(8,128)} %get-tuple-element.18) | copy-start | bytes 3145732
  210.6 0.8 copy-start.2
  210.6 1.0 copy-start.3
where the time goes:
time: 237 us
  Pallas kernels  215 us (91%)
  waiting for transfers between devices  16.8 us (7%)
    pallas_call x1, Pallas kernels, run_group(): pl.pallas_call(functools.partial(group_kernel, shard_rows, tall), out_sha...  162 us
    pallas_call x1, Pallas kernels, table_grad(): pl.pallas_call(functools.partial(table_kernel, tall), out_shape=jax.Shape...  25.3 us
    pallas_call x1, Pallas kernels, finish_weights(): pl.pallas_call(weights_kernel, out_shape=(jax.ShapeDtypeStruct(p1.shape,...  17.9 us
    ppermute x1, waiting for transfers between devices, per_device(): far_x = lax.ppermute(far, 'tensor', over_y)  12.9 us
    pallas_call x1, Pallas kernels, look_up(): pl.pallas_call(functools.partial(lookup_kernel, shard_rows), out_shape=ja...  9.84 us
  transfers between devices with their start and end apart: 4, of which 2 were waited for; matrix products, arithmetic and copies ran while one was open for 0% of the time, Pallas kernels for 8%

commit v1 on v0

--- a/solution.py
+++ b/solution.py
@@ -45,12 +45,11 @@
     loop(0, total // 16, lambda j: body(pl.multiple_of(j * 16, 16)))
 
 
-def sort_keys(ids, keys, place, ordered, first, shard_rows, tall, rank0):
+def make_keys(ids, keys, shard_rows, rank0):
     reps, per, _ = ids.shape
     count = reps * per * LANES
     t = per * LANES // 4
     shift = t.bit_length() - 1
-    lines = reps * per
     lane = lax.broadcasted_iota(I32, (per, LANES), 1)
     spot = lax.broadcasted_iota(I32, (per, LANES), 0) * LANES + lane
     block = jnp.right_shift(spot, shift)
@@ -59,40 +58,44 @@
         row = ids[k] - rank0
         row = jnp.where((row >= 0) & (row < shard_rows), row, shard_rows)
         keys[k * per : (k + 1) * per, :] = (row * count + (k * per * LANES + kept)).astype(F32)
+
+
+def columns(refs, b):
+    same = lax.broadcasted_iota(I32, (LANES, LANES), 0) == lax.broadcasted_iota(I32, (LANES, LANES), 1)
+    wide = (jnp.where(same, jnp.broadcast_to(ref[pl.ds(b, 1), :], (LANES, LANES)), 0.0) for ref in refs)
+    return [jnp.sum(w, axis=1, keepdims=True) for w in wide]
+
+
+def count_below(keys, place):
+    lines = keys.shape[0]
     place[...] = jnp.zeros_like(place)
+
+    def some(j):
+        cols = [columns((keys,), 4 * j + u)[0] for u in range(4)]
+        for a in range(lines):
+            row = keys[a : a + 1, :]
+            hits = sum(jnp.where(col < row, 1.0, 0.0) for col in cols)
+            place[a : a + 1, :] += jnp.sum(hits, axis=0, keepdims=True)
+
+    loop(0, lines // 4, some)
+
+
+def put_in_order(keys, place, ordered, first, tall):
+    lines = keys.shape[0]
     ordered[...] = jnp.zeros_like(ordered)
-    up = lax.broadcasted_iota(I32, (LANES, LANES), 0)
-    over = lax.broadcasted_iota(I32, (LANES, LANES), 1)
-    same = up == over
-    overf = over.astype(F32)
-
-    def column(ref, b):
-        return jnp.sum(jnp.where(same, jnp.broadcast_to(ref[pl.ds(b, 1), :], (LANES, LANES)), 0.0), axis=1, keepdims=True)
-
-    def count_below(b):
-        col = column(keys, b)
-
-        def one(a):
-            at = pl.ds(a, 1)
-            place[at, :] += jnp.sum(jnp.where(col < keys[at, :], 1.0, 0.0), axis=0, keepdims=True)
-
-        loop(0, lines, one)
-
-    loop(0, lines, count_below)
-
-    def put(b):
-        col, spot_of = column(keys, b), column(place, b)
-
-        def one(a):
-            want = overf + (a * LANES).astype(F32)
-            ordered[pl.ds(a, 1), :] += jnp.sum(jnp.where(spot_of == want, col, 0.0), axis=0, keepdims=True)
-
-        loop(0, lines, one)
-        edge = overf * float(tall * count)
-        first[...] += jnp.sum(jnp.where(col < edge, 1.0, 0.0), axis=0, keepdims=True)
-
     first[...] = jnp.zeros_like(first)
-    loop(0, lines, put)
+    lane = lax.broadcasted_iota(I32, (1, LANES), 1).astype(F32)
+    edge = lane * float(tall * lines * LANES)
+
+    def some(j):
+        cols = [columns((keys, place), 4 * j + u) for u in range(4)]
+        for a in range(lines):
+            want = lane + float(a * LANES)
+            hits = sum(jnp.where(spot == want, key, 0.0) for key, spot in cols)
+            ordered[a : a + 1, :] += jnp.sum(hits, axis=0, keepdims=True)
+        first[...] += jnp.sum(sum(jnp.where(key < edge, 1.0, 0.0) for key, _ in cols), axis=0, keepdims=True)
+
+    loop(0, lines // 4, some)
 
 
 def group_kernel(shard_rows, tall, ids_ref, xm_hbm, w1_hbm, w2_hbm, g_ref, do_hbm,
@@ -205,6 +208,10 @@
         x_part(q).start()
     d_across(z, start)
 
+    for k in range(3):
+        arrived(idl.at[order[k]], R_IDS + order[k])
+    make_keys(idl, keys, shard_rows, r * shard_rows)
+    count_below(keys, place)
     d_got(0)
 
     @pl.when(middle)
@@ -239,6 +246,9 @@
         n_own(q, start)
         if q == XQ // 2 - 1:
             n_along(0, start)
+            put_in_order(keys, place, ordered, first, tall)
+            ord_o[...] = ordered[...].astype(I32)
+            first_o[...] = first[...].astype(I32)
 
             @pl.when(middle)
             def _():
@@ -489,13 +499,6 @@
     local(dxo, blk(dx_o, z, c, y), L_DX).wait()
     dx_hand(z)
     dx_hand(order[0])
-
-    for k in range(3):
-        arrived(idl.at[order[k]], R_IDS + order[k])
-    sort_keys(idl, keys, place, ordered, first, shard_rows, tall, r * shard_rows)
-    ord_o[...] = ordered[...].astype(I32)
-    first_o[...] = first[...].astype(I32)
-
     for i in (n2 - 2, n2 - 1):
         flush(i, pd, dw2_o)[1].wait()
     if f % tw:

time: 237 us -> 230 us (0.970)
  Pallas kernels: 215 us -> 208 us
    pallas_call x1, Pallas kernels: 162 us -> 155 us  [run_group(): pl.pallas_call(functools.partial(group_kernel, shard_rows, tall), out_sha...]
where the time goes in v1:
time: 230 us
  Pallas kernels  208 us (90%)
  waiting for transfers between devices  16.8 us (7%)
    pallas_call x1, Pallas kernels, run_group(): pl.pallas_call(functools.partial(group_kernel, shard_rows, tall), out_sha...  155 us
    pallas_call x1, Pallas kernels, table_grad(): pl.pallas_call(functools.partial(table_kernel, tall), out_shape=jax.Shape...  25.3 us
    pallas_call x1, Pallas kernels, finish_weights(): pl.pallas_call(weights_kernel, out_shape=(jax.ShapeDtypeStruct(p1.shape,...  17.9 us
    ppermute x1, waiting for transfers between devices, per_device(): far_x = lax.ppermute(far, 'tensor', over_y)  12.9 us
    pallas_call x1, Pallas kernels, look_up(): pl.pallas_call(functools.partial(lookup_kernel, shard_rows), out_shape=ja...  9.84 us
  transfers between devices with their start and end apart: 4, of which 2 were waited for; matrix products, arithmetic and copies ran while one was open for 0% of the time, Pallas kernels for 8%

profile of v1, /device:TPU:0, one launch (start us, length us, event | category | flops | bytes accessed | tf_op | source)
XLA Modules:
  0.0 229.9 jit_solution(6618172651943979735)
XLA Ops:
  0.6 9.8 %look_up.1.xm_hbm = bf16[512,2048]{1,0:T(8,128)(2,1)} custom-call(s32[4,128]{1,0:T(4,128)} %bitcast.6, s32[4,128]{1,0:T(4,128)} %bitcast.7, bf16[1000,8,2048]{2,1,0:T(8,128)(2,1)} %bitcast.5), custom_call_target="tpu_custom_call" | custom-call | flops 16777216 | bytes 20971520 | tf_op jit(solution)/shard_map/look_up/pallas_call | solution.py:634
  10.5 155.1 %group_step.1 = (f32[128,2048]{1,0:T(8,128)}, f32[128,2048]{1,0:T(8,128)}, s32[16,128]{1,0:T(8,128)}, s32[1,128]{1,0:T(1,128)}, bf16[2048,2048]{1,0:T(8,128)(2,1...) custom-call(s32[4,128]{1,0:T(4,128)} %bitcast.8, ...), custom_call_target="tpu_custom_call" | custom-call | flops 53150220288 | bytes 268435456 | tf_op jit(solution)/shard_map/group_step/pallas_call | solution.py:558
  165.6 0.1 collective-permute-start.1
  165.7 0.4 collective-permute-start.2
  166.1 1.7 collective-permute-start
  167.8 12.9 %collective-permute-done.1.far_across = bf16[128,2048]{1,0:T(8,128)(2,1)S(1)} collective-permute-done((bf16[128,2048]{1,0:T(8,128)(2,1)}, bf16[128,2048]{1,0:T(8,128)(2,1)S(1)}, u32[]{:S(2)}, u32[]{:S(2)}) %collective-permute-start.1) | collective-permute-done | bytes 524320 | tf_op jit(solution)/shard_map/ppermute | solution.py:806
  180.7 0.0 copy-start.1
  180.7 0.0 collective-permute-start.3
  180.7 0.0 copy-start
  180.7 17.9 %finish_weights.1 = (f32[2048,1408]{1,0:T(8,128)}, f32[1408,2048]{1,0:T(8,128)}) custom-call(f32[2048,1408]{1,0:T(8,128)} %get-tuple-element.24.p1, f32[1408,2048]{1,0:T(8,128)} %get-tuple-element.25.p2, bf16[512,2048]{1,0:T(8,128)(2,1)} %get-tuple-element.26.nk_in, bf16[512,2048]{1,0:T(8,128)(2,1)} %get-tuple-element.27.dk_in, ...), custom_call_target="tpu_custom_call" | custom-call | flops 23068672000 | bytes 57671680 | tf_op jit(solution)/shard_map/finish_weights/pallas_call | solution.py:699
  198.6 0.0 copy-done.1
  198.6 4.0 %collective-permute-done = f32[128,2048]{1,0:T(8,128)S(1)} collective-permute-done((f32[128,2048]{1,0:T(8,128)}, f32[128,2048]{1,0:T(8,128)S(1)}, u32[]{:S(2)}, u32[]{:S(2)}) %collective-permute-start) | collective-permute-done | bytes 1048608 | tf_op jit(solution)/shard_map/ppermute | solution.py:808
  202.6 0.0 copy-done
  202.6 0.9 add_convert_fusion
  203.5 0.0 collective-permute-done.2.far_partner
  203.5 0.0 copy-start.2
  203.5 0.0 collective-permute-done.3.far_both
  203.5 0.0 copy-start.3
  203.5 0.8 copy-done.2
  204.3 0.2 copy-done.3
  204.5 25.3 %table_grad.1 = f32[8000,2048]{1,0:T(8,128)} custom-call(s32[2048]{0:T(1024)} %bitcast.10, s32[128]{0:T(128)} %bitcast.11, bf16[2048,2048]{1,0:T(8,128)(2,1)} %get-tuple-element.22.dx_in, bf16[128,2048]{1,0:T(8,128)(2,1)} %get-tuple-element.23.far_own, bf16[128,2048]{1,0:T(8,128)(2,1)} %copy-done.1, bf16[128,2048]{1,0:T(8,128)(2,1)} %copy-done.2, ...), custom_call_target="tpu_custom_call" | custom-call | flops 26214400000 | bytes 65536000 | tf_op jit(solution)/shard_map/table_grad/pallas_call | solution.py:774
Async XLA Ops:
  165.6 15.1 %collective-permute-start.1 = (bf16[128,2048]{1,0:T(8,128)(2,1)}, bf16[128,2048]{1,0:T(8,128)(2,1)S(1)}, u32[]{:S(2)}, u32[]{:S(2)}) collective-permute-start(bf16[128,2048]{1,0:T(8,128)(2,1)} %get-tuple-element.23.far_own), channel_id=1, source_target_pairs={{0,2},{1,3},{2,0},{3,1},{4,6},{5,7},{6,4},{7,5},{8,10},{9,11},{10,... | collective-permute-start | bytes 1572872 | tf_op jit(solution)/shard_map/ppermute | solution.py:806
  165.7 37.8 %collective-permute-start.2 = (bf16[128,2048]{1,0:T(8,128)(2,1)}, bf16[128,2048]{1,0:T(8,128)(2,1)S(1)}, u32[]{:S(2)}, u32[]{:S(2)}) collective-permute-start(bf16[128,2048]{1,0:T(8,128)(2,1)} %get-tuple-element.23.far_own), channel_id=1, source_target_pairs={{0,1},{1,0},{2,3},{3,2},{4,5},{5,4},{6,7},{7,6},{8,9},{9,8},{10,11... | collective-permute-start | bytes 1572872 | tf_op jit(solution)/shard_map/ppermute | solution.py:807
  166.1 36.4 %collective-permute-start = (f32[128,2048]{1,0:T(8,128)}, f32[128,2048]{1,0:T(8,128)S(1)}, u32[]{:S(2)}, u32[]{:S(2)}) collective-permute-start(f32[128,2048]{1,0:T(8,128)} %get-tuple-element.19), channel_id=1, source_target_pairs={{0,2},{1,3},{2,0},{3,1},{4,6},{5,7},{6,4},{7,5},{8,10},{9,11},{10,... | collective-permute-start | bytes 3145736 | tf_op jit(solution)/shard_map/ppermute | solution.py:808
  180.7 17.9 %copy-start.1 = (bf16[128,2048]{1,0:T(8,128)(2,1)}, bf16[128,2048]{1,0:T(8,128)(2,1)S(1)}, u32[]{:S(2)}) copy-start(bf16[128,2048]{1,0:T(8,128)(2,1)S(1)} %collective-permute-done.1.far_across) | copy-start | bytes 1572868
  180.7 22.8 %collective-permute-start.3 = (bf16[128,2048]{1,0:T(8,128)(2,1)S(1)}, bf16[128,2048]{1,0:T(8,128)(2,1)S(1)}, u32[]{:S(2)}, u32[]{:S(2)}) collective-permute-start(bf16[128,2048]{1,0:T(8,128)(2,1)S(1)} %collective-permute-done.1.far_across), channel_id=1, source_target_pairs={{0,1},{1,0},{2,3},{3,2},{4,5},{5,4},{6,7},{7,6},{8,9},{9,8},{10,11... | collective-permute-start | bytes 1572872 | tf_op jit(solution)/shard_map/ppermute | solution.py:810
  180.7 21.9 %copy-start = (f32[128,2048]{1,0:T(8,128)S(1)}, f32[128,2048]{1,0:T(8,128)}, u32[]{:S(2)}) copy-start(f32[128,2048]{1,0:T(8,128)} %get-tuple-element.18) | copy-start | bytes 3145732
  203.5 0.8 copy-start.2
  203.5 1.0 copy-start.3

commit v2 on v1

--- a/solution.py
+++ b/solution.py
@@ -20,9 +20,9 @@
 PQ = 4
 
 R_IDS, R_DZ, R_DY, R_DC, R_NZ, R_NC, R_XZ, R_XY, R_XC = 0, 4, 8, 12, 16, 24, 28, 36, 44
-R_XM, R_X, R_NO, R_PC, R_PY, N_R = 48, 52, 56, 60, 68, 72
+R_XM, R_X, R_NO, R_PC, R_PY, R_NY, N_R = 48, 52, 56, 60, 68, 72, 73
 S_IDS, S_DZ, S_DY, S_DC, S_NZ, S_NC, S_XZ, S_XY, S_XC = 0, 3, 8, 12, 16, 26, 30, 40, 48
-S_XM, S_X, S_NO, S_PC, S_PY, N_S = 52, 56, 60, 64, 72, 76
+S_XM, S_X, S_NO, S_PC, S_PY, S_NY, N_S = 52, 56, 60, 64, 72, 76, 77
 L_W1, L_W2, L_XM, L_DX, L_YS, L_YB, L_DW, L_DO, L_K, N_L = 0, 1, 2, 3, 4, 5, 6, 8, 9, 13
 
 
@@ -349,13 +349,25 @@
     for q in range(PQ):
         part_pair(pf, rf, 1, q).wait_send()
 
+    th = t // 2
+
+    def n_parts(k, lands):
+        own, other = blk(n, order[k], c, y), blk(n, order[k], c, 1 - y)
+        if lands == 2:
+            other = other.at[pl.ds(0, th)]
+        return (own, y), (other, 1 - y)
+
     def n_got(k):
-        for b in range(2):
-            arrived(blk(n, order[k], c, b), R_NZ + 4 * b + order[k])
-
-    def n_on(k):
-        for b in range(2):
-            pass_on(k, blk(n, order[k], c, b), S_NZ + 5 * b, R_NZ + 4 * b, start)
+        for ref, b in n_parts(k, k):
+            arrived(ref, R_NZ + 4 * b + order[k])
+
+    def n_on(k, act):
+        for ref, b in n_parts(k, 1 if k == 1 else 2):
+            pass_on(k, ref, S_NZ + 5 * b, R_NZ + 4 * b, act)
+
+    def n_cross(act):
+        half_own = blk(n, order[2], c, y).at[pl.ds(th, th)]
+        act(remote(half_own, half_own, S_NY, R_NY, across))
 
     def n_pair(zz, act):
         act(remote(duo(n, zz, c), duo(n, zz, c), S_NC + zz, R_NC + zz, partner))
@@ -365,9 +377,9 @@
 
     @pl.when(middle)
     def _():
-        n_on(0)
+        n_on(0, start)
         n_got(1)
-        n_on(1)
+        n_on(1, start)
         n_pair(order[1], start)
 
     def unit(k, slopes):
@@ -379,11 +391,15 @@
         arrived(duo(d, zz, 1 - c), R_DC + zz)
         grad_hidden(zz, slopes)
 
-    def n_rest(k, on):
-        n_got(k)
+    def n_far(on):
+        n_got(2)
         if on:
-            n_on(k)
-        n_pair(order[k], start)
+            n_on(2, start)
+        n_cross(start)
+
+    def n_far_pair():
+        arrived(blk(n, order[2], c, 1 - y).at[pl.ds(th, th)], R_NY)
+        n_pair(order[2], start)
 
     unit(0, pf)
 
@@ -401,7 +417,6 @@
         dxo[at, :] = (d[pl.ds(row(z, c, y) + i, 16), :].astype(F32) + dxn).astype(BF16)
 
     rows_loop(t, grad_x)
-    th = t // 2
 
     def dx_part(zz, yy, h):
         return dx_o.at[pl.ds(pl.multiple_of(row(zz, c, yy) + h * th, th), th)]
@@ -453,9 +468,14 @@
     for q in range(PQ):
         part_pair(pd, rd, 0, q).wait_send()
 
-    pl.when(middle)(lambda: n_rest(2, True))
+    pl.when(middle)(lambda: n_far(True))
     dx_along(start)
-    pl.when(end)(lambda: n_rest(1, False))
+
+    @pl.when(end)
+    def _():
+        n_got(1)
+        n_pair(order[1], start)
+
     unit(1, pd)
 
     @pl.when(middle)
@@ -480,10 +500,12 @@
         here[...] = lax.dot_general(lhs[early_rows, at], rhs[early_rows, :], TN, preferred_element_type=F32)
         out.start()
 
-    loop(0, n1, lambda i: weight_tile(i, n, dus, pf, dw1_o))
+    loop(0, n1 // 2, lambda i: weight_tile(i, n, dus, pf, dw1_o))
+    pl.when(end)(lambda: n_far(False))
+    loop(n1 // 2, n1, lambda i: weight_tile(i, n, dus, pf, dw1_o))
     for i in (n1 - 2, n1 - 1):
         flush(i, pf, dw1_o)[1].wait()
-    pl.when(end)(lambda: n_rest(2, False))
+    n_far_pair()
     unit(2, pd)
     kept = [
         local(src.at[late_rows], dst, L_K + i)
@@ -533,13 +555,14 @@
     def _():
         for k in range(3):
             pass_on(k, blk(d, order[k], c, y), S_DZ, R_DZ, sent)
+            n_on(k, sent)
             for b in range(2):
                 pass_on(k, dx_next(k, b), S_XZ + 5 * b, R_XZ + 4 * b, sent)
-                pass_on(k, blk(n, order[k], c, b), S_NZ + 5 * b, R_NZ + 4 * b, sent)
 
     for q in range(XQ):
         xm_part(q).wait_send()
         n_own(q, sent)
+    n_cross(sent)
     for q in range(PQ):
         part_across(q).wait_send()
     for zz in (z, *order[:2]):
@@ -721,14 +744,17 @@
         at = pl.ds(pl.multiple_of(late * (4 * t) + k * (2 * t), t), 2 * t)
         return at, pltpu.make_async_copy(dx_in.at[at], dxb.at[at], dx_sem.at[k])
 
-    def far(k, src, cc, yy):
-        at = pl.ds(pl.multiple_of((1 - late) * (12 * t) + cc * (2 * t) + yy * t, t), t)
-        return at, pltpu.make_async_copy(src, dxb.at[at], dx_sem.at[6 + k])
-
-    fars = ((far_own, c, y), (far_across, c, 1 - y), (far_partner, 1 - c, y), (far_both, 1 - c, 1 - y))
+    def far(cc, yy):
+        return pl.multiple_of((1 - late) * (12 * t) + cc * (2 * t) + yy * t, t)
+
     loop(0, 6, lambda k: near(k)[1].start())
-    for k, what in enumerate(fars):
-        far(k, *what)[1].start()
+    for src, cc, yy in ((far_own, c, y), (far_across, c, 1 - y), (far_partner, 1 - c, y), (far_both, 1 - c, 1 - y)):
+        to = far(cc, yy)
+
+        def widen_far(i, src=src, to=to):
+            dxf[pl.ds(to + i, 16), :] = src[pl.ds(i, 16), :].astype(F32)
+
+        rows_loop(t, widen_far)
 
     def widen_piece(at, cp):
         cp.wait()
@@ -740,8 +766,6 @@
         rows_loop(at.size, widen)
 
     loop(0, 6, lambda k: widen_piece(*near(k)))
-    for k, what in enumerate(fars):
-        widen_piece(*far(k, *what))
 
     def tile_out(i):
         slot = lax.rem(i, RING)
@@ -777,13 +801,13 @@
         grid_spec=pltpu.PrefetchScalarGridSpec(
             num_scalar_prefetch=2,
             grid=(1,),
-            in_specs=[any_] * 5,
+            in_specs=[any_, *[pl.BlockSpec(memory_space=pltpu.VMEM)] * 4],
             out_specs=any_,
             scratch_shapes=[
-                V((count, m), BF16), V((count, m), F32), V((RING, tall, m), F32), S((10,)), S((RING,)),
+                V((count, m), BF16), V((count, m), F32), V((RING, tall, m), F32), S((6,)), S((RING,)),
             ],
         ),
-        compiler_params=pltpu.CompilerParams(vmem_limit_bytes=60 << 20),
+        compiler_params=pltpu.CompilerParams(vmem_limit_bytes=44 << 20),
         cost_estimate=pl.CostEstimate(flops=16000 * shard_rows * m // 10, bytes_accessed=4 * shard_rows * m, transcendentals=0),
         name="table_grad",
     )(ordered, first, dx_all, *fars)

time: 230 us -> 234 us (1.017)
  Pallas kernels: 208 us -> 212 us
    pallas_call x1, Pallas kernels: 155 us -> 159 us  [run_group(): pl.pallas_call(functools.partial(group_kernel, shard_rows, tall), out_sha...]
  transfers between devices with their start and end apart: 4 -> 4, of which waited for: 2 -> 2; matrix products, arithmetic and copies ran while one was open for 0% -> 1% of each run, Pallas kernels for 8% -> 8%
where the time goes in v2:
time: 234 us
  Pallas kernels  212 us (91%)
  waiting for transfers between devices  17 us (7%)
    pallas_call x1, Pallas kernels, run_group(): pl.pallas_call(functools.partial(group_kernel, shard_rows, tall), out_sha...  159 us
    pallas_call x1, Pallas kernels, table_grad(): pl.pallas_call(functools.partial(table_kernel, tall), out_shape=jax.Shape...  24.7 us
    pallas_call x1, Pallas kernels, finish_weights(): pl.pallas_call(weights_kernel, out_shape=(jax.ShapeDtypeStruct(p1.shape,...  17.8 us
    ppermute x1, waiting for transfers between devices, per_device(): far_x = lax.ppermute(far, 'tensor', over_y)  12.9 us
    pallas_call x1, Pallas kernels, look_up(): pl.pallas_call(functools.partial(lookup_kernel, shard_rows), out_shape=ja...  9.84 us
  transfers between devices with their start and end apart: 4, of which 2 were waited for; matrix products, arithmetic and copies ran while one was open for 1% of the time, Pallas kernels for 8%

profile of v2, /device:TPU:0, one launch (start us, length us, event | category | flops | bytes accessed | tf_op | source)
XLA Modules:
  0.0 234.0 jit_solution(17727997438140626595)
XLA Ops:
  0.6 9.8 %look_up.1.xm_hbm = bf16[512,2048]{1,0:T(8,128)(2,1)} custom-call(s32[4,128]{1,0:T(4,128)} %bitcast.8, s32[4,128]{1,0:T(4,128)} %bitcast.9, bf16[1000,8,2048]{2,1,0:T(8,128)(2,1)} %bitcast.7), custom_call_target="tpu_custom_call" | custom-call | flops 16777216 | bytes 20971520 | tf_op jit(solution)/shard_map/look_up/pallas_call | solution.py:657
  10.5 159.4 %group_step.1 = (f32[128,2048]{1,0:T(8,128)}, f32[128,2048]{1,0:T(8,128)}, s32[16,128]{1,0:T(8,128)}, s32[1,128]{1,0:T(1,128)}, bf16[2048,2048]{1,0:T(8,128)(2,1...) custom-call(s32[4,128]{1,0:T(4,128)} %bitcast.10, ...), custom_call_target="tpu_custom_call" | custom-call | flops 53150220288 | bytes 268435456 | tf_op jit(solution)/shard_map/group_step/pallas_call | solution.py:581
  169.9 0.1 collective-permute-start.1
  170.0 0.4 collective-permute-start.2
  170.4 1.7 collective-permute-start
  172.1 12.9 %collective-permute-done.1.far_across = bf16[128,2048]{1,0:T(8,128)(2,1)S(1)} collective-permute-done((bf16[128,2048]{1,0:T(8,128)(2,1)}, bf16[128,2048]{1,0:T(8,128)(2,1)S(1)}, u32[]{:S(2)}, u32[]{:S(2)}) %collective-permute-start.1) | collective-permute-done | bytes 524320 | tf_op jit(solution)/shard_map/ppermute | solution.py:830
  185.0 0.0 collective-permute-start.3
  185.0 0.0 copy-start.3
  185.0 0.0 copy-start
  185.0 0.0 copy-start.1
  185.0 0.0 copy-start.2
  185.0 17.8 %finish_weights.1 = (f32[2048,1408]{1,0:T(8,128)}, f32[1408,2048]{1,0:T(8,128)}) custom-call(f32[2048,1408]{1,0:T(8,128)} %get-tuple-element.24.p1, f32[1408,2048]{1,0:T(8,128)} %get-tuple-element.25.p2, bf16[512,2048]{1,0:T(8,128)(2,1)} %get-tuple-element.26.nk_in, bf16[512,2048]{1,0:T(8,128)(2,1)} %get-tuple-element.27.dk_in, ...), custom_call_target="tpu_custom_call" | custom-call | flops 23068672000 | bytes 57671680 | tf_op jit(solution)/shard_map/finish_weights/pallas_call | solution.py:722
  202.8 4.2 %collective-permute-done = f32[128,2048]{1,0:T(8,128)} collective-permute-done((f32[128,2048]{1,0:T(8,128)}, f32[128,2048]{1,0:T(8,128)}, u32[]{:S(2)}, u32[]{:S(2)}) %collective-permute-start) | collective-permute-done | bytes 1048608 | tf_op jit(solution)/shard_map/ppermute | solution.py:832
  206.9 0.0 copy-done.3
  206.9 2.2 add_convert_fusion
  209.1 0.0 collective-permute-done.2.far_partner
  209.1 0.0 collective-permute-done.3.far_both
  209.1 0.0 copy-done
  209.1 0.0 copy-done.1
  209.1 0.0 copy-done.2
  209.1 24.7 %table_grad.1 = f32[8000,2048]{1,0:T(8,128)} custom-call(s32[2048]{0:T(1024)S(1)} %bitcast.5, s32[128]{0:T(128)S(1)} %bitcast.6, bf16[2048,2048]{1,0:T(8,128)(2,1)} %get-tuple-element.22.dx_in, bf16[128,2048]{1,0:T(8,128)(2,1)S(1)} %copy-done, bf16[128,2048]{1,0:T(8,128)(2,1)S(1)} %collective-permute-done.1.far_across, ...), custom_call_target="tpu_custom_call" | custom-call | flops 26214400000 | bytes 65536000 | tf_op jit(solution)/shard_map/table_grad/pallas_call | solution.py:798
Async XLA Ops:
  169.9 15.1 %collective-permute-start.1 = (bf16[128,2048]{1,0:T(8,128)(2,1)}, bf16[128,2048]{1,0:T(8,128)(2,1)S(1)}, u32[]{:S(2)}, u32[]{:S(2)}) collective-permute-start(bf16[128,2048]{1,0:T(8,128)(2,1)} %get-tuple-element.23.far_own), channel_id=1, source_target_pairs={{0,2},{1,3},{2,0},{3,1},{4,6},{5,7},{6,4},{7,5},{8,10},{9,11},{10,... | collective-permute-start | bytes 1572872 | tf_op jit(solution)/shard_map/ppermute | solution.py:830
  170.0 39.1 %collective-permute-start.2 = (bf16[128,2048]{1,0:T(8,128)(2,1)}, bf16[128,2048]{1,0:T(8,128)(2,1)S(1)}, u32[]{:S(2)}, u32[]{:S(2)}) collective-permute-start(bf16[128,2048]{1,0:T(8,128)(2,1)} %get-tuple-element.23.far_own), channel_id=1, source_target_pairs={{0,1},{1,0},{2,3},{3,2},{4,5},{5,4},{6,7},{7,6},{8,9},{9,8},{10,11... | collective-permute-start | bytes 1572872 | tf_op jit(solution)/shard_map/ppermute | solution.py:831
  170.4 36.5 %collective-permute-start = (f32[128,2048]{1,0:T(8,128)}, f32[128,2048]{1,0:T(8,128)}, u32[]{:S(2)}, u32[]{:S(2)}) collective-permute-start(f32[128,2048]{1,0:T(8,128)} %get-tuple-element.19), channel_id=1, source_target_pairs={{0,2},{1,3},{2,0},{3,1},{4,6},{5,7},{6,4},{7,5},{8,10},{9,11},{10,... | collective-permute-start | bytes 3145736 | tf_op jit(solution)/shard_map/ppermute | solution.py:832
  185.0 24.2 %collective-permute-start.3 = (bf16[128,2048]{1,0:T(8,128)(2,1)S(1)}, bf16[128,2048]{1,0:T(8,128)(2,1)S(1)}, u32[]{:S(2)}, u32[]{:S(2)}) collective-permute-start(bf16[128,2048]{1,0:T(8,128)(2,1)S(1)} %collective-permute-done.1.far_across), channel_id=1, source_target_pairs={{0,1},{1,0},{2,3},{3,2},{4,5},{5,4},{6,7},{7,6},{8,9},{9,8},{10,11... | collective-permute-start | bytes 1572872 | tf_op jit(solution)/shard_map/ppermute | solution.py:834
  185.0 22.0 %copy-start.3 = (f32[128,2048]{1,0:T(8,128)S(1)}, f32[128,2048]{1,0:T(8,128)}, u32[]{:S(2)}) copy-start(f32[128,2048]{1,0:T(8,128)} %get-tuple-element.18) | copy-start | bytes 3145732
  185.0 24.2 %copy-start = (bf16[128,2048]{1,0:T(8,128)(2,1)S(1)}, bf16[128,2048]{1,0:T(8,128)(2,1)}, u32[]{:S(2)}) copy-start(bf16[128,2048]{1,0:T(8,128)(2,1)} %get-tuple-element.23.far_own) | copy-start | bytes 1572868
  185.0 24.2 %copy-start.1 = (s32[16,128]{1,0:T(8,128)S(1)}, s32[16,128]{1,0:T(8,128)}, u32[]{:S(2)}) copy-start(s32[16,128]{1,0:T(8,128)} %get-tuple-element.20) | copy-start | bytes 24580
  185.0 24.2 %copy-start.2 = (s32[1,128]{1,0:T(1,128)S(1)}, s32[1,128]{1,0:T(1,128)}, u32[]{:S(2)}) copy-start(s32[1,128]{1,0:T(1,128)} %get-tuple-element.21) | copy-start | bytes 1540

commit v3 on v2

--- a/solution.py
+++ b/solution.py
@@ -382,20 +382,24 @@
         n_on(1, start)
         n_pair(order[1], start)
 
-    def unit(k, slopes):
+    def unit(k, slopes, between=None):
         zz = order[k]
         arrived(blk(d, zz, c, 1 - y), R_DY + zz)
         d_pair(zz, start)
         arrived(duo(n, zz, 1 - c), R_NC + zz)
+        if between:
+            between()
         hidden(zz, slopes)
         arrived(duo(d, zz, 1 - c), R_DC + zz)
         grad_hidden(zz, slopes)
 
-    def n_far(on):
-        n_got(2)
+    def n_far(part, on):
+        ref, b = n_parts(2, 2)[part]
+        arrived(ref, R_NZ + 4 * b + order[2])
         if on:
-            n_on(2, start)
-        n_cross(start)
+            pass_on(2, ref, S_NZ + 5 * b, R_NZ + 4 * b, start)
+        if part == 0:
+            n_cross(start)
 
     def n_far_pair():
         arrived(blk(n, order[2], c, 1 - y).at[pl.ds(th, th)], R_NY)
@@ -468,7 +472,12 @@
     for q in range(PQ):
         part_pair(pd, rd, 0, q).wait_send()
 
-    pl.when(middle)(lambda: n_far(True))
+
+    @pl.when(middle)
+    def _():
+        n_far(0, True)
+        n_far(1, True)
+
     dx_along(start)
 
     @pl.when(end)
@@ -477,6 +486,7 @@
         n_pair(order[1], start)
 
     unit(1, pd)
+    pl.when(end)(lambda: n_far(0, False))
 
     @pl.when(middle)
     def _():
@@ -501,19 +511,18 @@
         out.start()
 
     loop(0, n1 // 2, lambda i: weight_tile(i, n, dus, pf, dw1_o))
-    pl.when(end)(lambda: n_far(False))
+    pl.when(end)(lambda: n_far(1, False))
     loop(n1 // 2, n1, lambda i: weight_tile(i, n, dus, pf, dw1_o))
     for i in (n1 - 2, n1 - 1):
         flush(i, pf, dw1_o)[1].wait()
     n_far_pair()
-    unit(2, pd)
+    unit(2, pd, lambda: pl.when(end)(lambda: dx_got(0, False)))
     kept = [
         local(src.at[late_rows], dst, L_K + i)
         for i, (src, dst) in enumerate(((n, nk_o), (d, dk_o), (hs, hk_o), (dus, duk_o)))
     ]
     for cp in kept:
         cp.start()
-    pl.when(end)(lambda: dx_got(0, False))
     pl.when(middle)(lambda: dx_got(2, True))
     loop(0, n2 // 2, lambda i: weight_tile(i, hs, d, pd, dw2_o))
     pl.when(end)(lambda: dx_got(1, False))

time: 234 us -> 227 us (0.970)
  Pallas kernels: 212 us -> 204 us
    pallas_call x1, Pallas kernels: 159 us -> 152 us  [run_group(): pl.pallas_call(functools.partial(group_kernel, shard_rows, tall), out_sha...]
where the time goes in v3:
time: 227 us; the launch traced here: 226 us
  Pallas kernels  204 us (90%)
  waiting for transfers between devices  17 us (7%)
    pallas_call x1, Pallas kernels, run_group(): pl.pallas_call(functools.partial(group_kernel, shard_rows, tall), out_sha...  152 us
    pallas_call x1, Pallas kernels, table_grad(): pl.pallas_call(functools.partial(table_kernel, tall), out_shape=jax.Shape...  24.7 us
    pallas_call x1, Pallas kernels, finish_weights(): pl.pallas_call(weights_kernel, out_shape=(jax.ShapeDtypeStruct(p1.shape,...  17.8 us
    ppermute x1, waiting for transfers between devices, per_device(): far_x = lax.ppermute(far, 'tensor', over_y)  12.9 us
    pallas_call x1, Pallas kernels, look_up(): pl.pallas_call(functools.partial(lookup_kernel, shard_rows), out_shape=ja...  9.84 us
  transfers between devices with their start and end apart: 4, of which 2 were waited for; matrix products, arithmetic and copies ran while one was open for 1% of the time, Pallas kernels for 8%

profile of v3, /device:TPU:0, one launch (start us, length us, event | category | flops | bytes accessed | tf_op | source)
XLA Modules:
  0.0 226.4 jit_solution(18406818295222186184)
XLA Ops:
  0.6 9.8 %look_up.1.xm_hbm = bf16[512,2048]{1,0:T(8,128)(2,1)} custom-call(s32[4,128]{1,0:T(4,128)} %bitcast.8, s32[4,128]{1,0:T(4,128)} %bitcast.9, bf16[1000,8,2048]{2,1,0:T(8,128)(2,1)} %bitcast.7), custom_call_target="tpu_custom_call" | custom-call | flops 16777216 | bytes 20971520 | tf_op jit(solution)/shard_map/look_up/pallas_call | solution.py:666
  10.5 151.9 %group_step.1 = (f32[128,2048]{1,0:T(8,128)}, f32[128,2048]{1,0:T(8,128)}, s32[16,128]{1,0:T(8,128)}, s32[1,128]{1,0:T(1,128)}, bf16[2048,2048]{1,0:T(8,128)(2,1...) custom-call(s32[4,128]{1,0:T(4,128)} %bitcast.10, ...), custom_call_target="tpu_custom_call" | custom-call | flops 53150220288 | bytes 268435456 | tf_op jit(solution)/shard_map/group_step/pallas_call | solution.py:590
  162.3 0.1 collective-permute-start.1
  162.4 0.4 collective-permute-start.2
  162.9 1.7 collective-permute-start
  164.5 12.9 %collective-permute-done.1.far_across = bf16[128,2048]{1,0:T(8,128)(2,1)S(1)} collective-permute-done((bf16[128,2048]{1,0:T(8,128)(2,1)}, bf16[128,2048]{1,0:T(8,128)(2,1)S(1)}, u32[]{:S(2)}, u32[]{:S(2)}) %collective-permute-start.1) | collective-permute-done | bytes 524320 | tf_op jit(solution)/shard_map/ppermute | solution.py:839
  177.4 0.0 collective-permute-start.3
  177.4 0.0 copy-start.3
  177.4 0.0 copy-start
  177.4 0.0 copy-start.1
  177.4 0.0 copy-start.2
  177.4 17.8 %finish_weights.1 = (f32[2048,1408]{1,0:T(8,128)}, f32[1408,2048]{1,0:T(8,128)}) custom-call(f32[2048,1408]{1,0:T(8,128)} %get-tuple-element.24.p1, f32[1408,2048]{1,0:T(8,128)} %get-tuple-element.25.p2, bf16[512,2048]{1,0:T(8,128)(2,1)} %get-tuple-element.26.nk_in, bf16[512,2048]{1,0:T(8,128)(2,1)} %get-tuple-element.27.dk_in, ...), custom_call_target="tpu_custom_call" | custom-call | flops 23068672000 | bytes 57671680 | tf_op jit(solution)/shard_map/finish_weights/pallas_call | solution.py:731
  195.2 4.2 %collective-permute-done = f32[128,2048]{1,0:T(8,128)} collective-permute-done((f32[128,2048]{1,0:T(8,128)}, f32[128,2048]{1,0:T(8,128)}, u32[]{:S(2)}, u32[]{:S(2)}) %collective-permute-start) | collective-permute-done | bytes 1048608 | tf_op jit(solution)/shard_map/ppermute | solution.py:841
  199.4 0.0 copy-done.3
  199.4 2.2 add_convert_fusion
  201.6 0.0 collective-permute-done.2.far_partner
  201.6 0.0 collective-permute-done.3.far_both
  201.6 0.0 copy-done
  201.6 0.0 copy-done.1
  201.6 0.0 copy-done.2
  201.6 24.7 %table_grad.1 = f32[8000,2048]{1,0:T(8,128)} custom-call(s32[2048]{0:T(1024)S(1)} %bitcast.5, s32[128]{0:T(128)S(1)} %bitcast.6, bf16[2048,2048]{1,0:T(8,128)(2,1)} %get-tuple-element.22.dx_in, bf16[128,2048]{1,0:T(8,128)(2,1)S(1)} %copy-done, bf16[128,2048]{1,0:T(8,128)(2,1)S(1)} %collective-permute-done.1.far_across, ...), custom_call_target="tpu_custom_call" | custom-call | flops 26214400000 | bytes 65536000 | tf_op jit(solution)/shard_map/table_grad/pallas_call | solution.py:807
Async XLA Ops:
  162.3 15.1 %collective-permute-start.1 = (bf16[128,2048]{1,0:T(8,128)(2,1)}, bf16[128,2048]{1,0:T(8,128)(2,1)S(1)}, u32[]{:S(2)}, u32[]{:S(2)}) collective-permute-start(bf16[128,2048]{1,0:T(8,128)(2,1)} %get-tuple-element.23.far_own), channel_id=1, source_target_pairs={{0,2},{1,3},{2,0},{3,1},{4,6},{5,7},{6,4},{7,5},{8,10},{9,11},{10,... | collective-permute-start | bytes 1572872 | tf_op jit(solution)/shard_map/ppermute | solution.py:839
  162.4 39.1 %collective-permute-start.2 = (bf16[128,2048]{1,0:T(8,128)(2,1)}, bf16[128,2048]{1,0:T(8,128)(2,1)S(1)}, u32[]{:S(2)}, u32[]{:S(2)}) collective-permute-start(bf16[128,2048]{1,0:T(8,128)(2,1)} %get-tuple-element.23.far_own), channel_id=1, source_target_pairs={{0,1},{1,0},{2,3},{3,2},{4,5},{5,4},{6,7},{7,6},{8,9},{9,8},{10,11... | collective-permute-start | bytes 1572872 | tf_op jit(solution)/shard_map/ppermute | solution.py:840
  162.9 36.5 %collective-permute-start = (f32[128,2048]{1,0:T(8,128)}, f32[128,2048]{1,0:T(8,128)}, u32[]{:S(2)}, u32[]{:S(2)}) collective-permute-start(f32[128,2048]{1,0:T(8,128)} %get-tuple-element.19), channel_id=1, source_target_pairs={{0,2},{1,3},{2,0},{3,1},{4,6},{5,7},{6,4},{7,5},{8,10},{9,11},{10,... | collective-permute-start | bytes 3145736 | tf_op jit(solution)/shard_map/ppermute | solution.py:841
  177.4 24.2 %collective-permute-start.3 = (bf16[128,2048]{1,0:T(8,128)(2,1)S(1)}, bf16[128,2048]{1,0:T(8,128)(2,1)S(1)}, u32[]{:S(2)}, u32[]{:S(2)}) collective-permute-start(bf16[128,2048]{1,0:T(8,128)(2,1)S(1)} %collective-permute-done.1.far_across), channel_id=1, source_target_pairs={{0,1},{1,0},{2,3},{3,2},{4,5},{5,4},{6,7},{7,6},{8,9},{9,8},{10,11... | collective-permute-start | bytes 1572872 | tf_op jit(solution)/shard_map/ppermute | solution.py:843
  177.4 22.0 %copy-start.3 = (f32[128,2048]{1,0:T(8,128)S(1)}, f32[128,2048]{1,0:T(8,128)}, u32[]{:S(2)}) copy-start(f32[128,2048]{1,0:T(8,128)} %get-tuple-element.18) | copy-start | bytes 3145732
  177.4 24.2 %copy-start = (bf16[128,2048]{1,0:T(8,128)(2,1)S(1)}, bf16[128,2048]{1,0:T(8,128)(2,1)}, u32[]{:S(2)}) copy-start(bf16[128,2048]{1,0:T(8,128)(2,1)} %get-tuple-element.23.far_own) | copy-start | bytes 1572868
  177.4 24.2 %copy-start.1 = (s32[16,128]{1,0:T(8,128)S(1)}, s32[16,128]{1,0:T(8,128)}, u32[]{:S(2)}) copy-start(s32[16,128]{1,0:T(8,128)} %get-tuple-element.20) | copy-start | bytes 24580
  177.4 24.2 %copy-start.2 = (s32[1,128]{1,0:T(1,128)S(1)}, s32[1,128]{1,0:T(1,128)}, u32[]{:S(2)}) copy-start(s32[1,128]{1,0:T(1,128)} %get-tuple-element.21) | copy-start | bytes 1540

commit v4 on v3

--- a/solution.py
+++ b/solution.py
@@ -382,13 +382,11 @@
         n_on(1, start)
         n_pair(order[1], start)
 
-    def unit(k, slopes, between=None):
+    def unit(k, slopes):
         zz = order[k]
         arrived(blk(d, zz, c, 1 - y), R_DY + zz)
         d_pair(zz, start)
         arrived(duo(n, zz, 1 - c), R_NC + zz)
-        if between:
-            between()
         hidden(zz, slopes)
         arrived(duo(d, zz, 1 - c), R_DC + zz)
         grad_hidden(zz, slopes)
@@ -515,21 +513,22 @@
     loop(n1 // 2, n1, lambda i: weight_tile(i, n, dus, pf, dw1_o))
     for i in (n1 - 2, n1 - 1):
         flush(i, pf, dw1_o)[1].wait()
+    pl.when(end)(lambda: dx_got(0, False))
     n_far_pair()
-    unit(2, pd, lambda: pl.when(end)(lambda: dx_got(0, False)))
+    local(dxo, blk(dx_o, z, c, y), L_DX).wait()
+    dx_hand(z)
+    pl.when(middle)(lambda: dx_got(2, True))
+    unit(2, pd)
+    pl.when(end)(lambda: dx_got(1, False))
     kept = [
         local(src.at[late_rows], dst, L_K + i)
         for i, (src, dst) in enumerate(((n, nk_o), (d, dk_o), (hs, hk_o), (dus, duk_o)))
     ]
     for cp in kept:
         cp.start()
-    pl.when(middle)(lambda: dx_got(2, True))
     loop(0, n2 // 2, lambda i: weight_tile(i, hs, d, pd, dw2_o))
-    pl.when(end)(lambda: dx_got(1, False))
+    dx_hand(order[0])
     loop(n2 // 2, n2, lambda i: weight_tile(i, hs, d, pd, dw2_o))
-    local(dxo, blk(dx_o, z, c, y), L_DX).wait()
-    dx_hand(z)
-    dx_hand(order[0])
     for i in (n2 - 2, n2 - 1):
         flush(i, pd, dw2_o)[1].wait()
     if f % tw:

time: 227 us -> 223 us (0.982)
  Pallas kernels: 204 us -> 200 us
    pallas_call x1, Pallas kernels: 152 us -> 148 us  [run_group(): pl.pallas_call(functools.partial(group_kernel, shard_rows, tall), out_sha...]
where the time goes in v4:
time: 223 us; the launch traced here: 222 us
  Pallas kernels  200 us (90%)
  waiting for transfers between devices  16.9 us (8%)
    pallas_call x1, Pallas kernels, run_group(): pl.pallas_call(functools.partial(group_kernel, shard_rows, tall), out_sha...  148 us
    pallas_call x1, Pallas kernels, table_grad(): pl.pallas_call(functools.partial(table_kernel, tall), out_shape=jax.Shape...  24.7 us
    pallas_call x1, Pallas kernels, finish_weights(): pl.pallas_call(weights_kernel, out_shape=(jax.ShapeDtypeStruct(p1.shape,...  17.8 us
    ppermute x1, waiting for transfers between devices, per_device(): far_x = lax.ppermute(far, 'tensor', over_y)  13 us
    pallas_call x1, Pallas kernels, look_up(): pl.pallas_call(functools.partial(lookup_kernel, shard_rows), out_shape=ja...  9.84 us
  transfers between devices with their start and end apart: 4, of which 2 were waited for; matrix products, arithmetic and copies ran while one was open for 1% of the time, Pallas kernels for 8%

profile of v4, /device:TPU:0, one launch (start us, length us, event | category | flops | bytes accessed | tf_op | source)
XLA Modules:
  0.0 222.4 jit_solution(15727433303158943146)
XLA Ops:
  0.6 9.8 %look_up.1.xm_hbm = bf16[512,2048]{1,0:T(8,128)(2,1)} custom-call(s32[4,128]{1,0:T(4,128)} %bitcast.8, s32[4,128]{1,0:T(4,128)} %bitcast.9, bf16[1000,8,2048]{2,1,0:T(8,128)(2,1)} %bitcast.7), custom_call_target="tpu_custom_call" | custom-call | flops 16777216 | bytes 20971520 | tf_op jit(solution)/shard_map/look_up/pallas_call | solution.py:665
  10.5 148.1 %group_step.1 = (f32[128,2048]{1,0:T(8,128)}, f32[128,2048]{1,0:T(8,128)}, s32[16,128]{1,0:T(8,128)}, s32[1,128]{1,0:T(1,128)}, bf16[2048,2048]{1,0:T(8,128)(2,1...) custom-call(s32[4,128]{1,0:T(4,128)} %bitcast.10, ...), custom_call_target="tpu_custom_call" | custom-call | flops 53150220288 | bytes 268435456 | tf_op jit(solution)/shard_map/group_step/pallas_call | solution.py:589
  158.6 0.3 collective-permute-start.1
  158.9 0.0 collective-permute-start.2
  158.9 1.8 collective-permute-start
  160.7 13.0 %collective-permute-done.1.far_across = bf16[128,2048]{1,0:T(8,128)(2,1)S(1)} collective-permute-done((bf16[128,2048]{1,0:T(8,128)(2,1)}, bf16[128,2048]{1,0:T(8,128)(2,1)S(1)}, u32[]{:S(2)}, u32[]{:S(2)}) %collective-permute-start.1) | collective-permute-done | bytes 524320 | tf_op jit(solution)/shard_map/ppermute | solution.py:838
  173.7 0.0 collective-permute-start.3
  173.7 0.0 copy-start.3
  173.7 0.0 copy-start
  173.7 0.0 copy-start.1
  173.7 0.0 copy-start.2
  173.7 17.8 %finish_weights.1 = (f32[2048,1408]{1,0:T(8,128)}, f32[1408,2048]{1,0:T(8,128)}) custom-call(f32[2048,1408]{1,0:T(8,128)} %get-tuple-element.24.p1, f32[1408,2048]{1,0:T(8,128)} %get-tuple-element.25.p2, bf16[512,2048]{1,0:T(8,128)(2,1)} %get-tuple-element.26.nk_in, bf16[512,2048]{1,0:T(8,128)(2,1)} %get-tuple-element.27.dk_in, ...), custom_call_target="tpu_custom_call" | custom-call | flops 23068672000 | bytes 57671680 | tf_op jit(solution)/shard_map/finish_weights/pallas_call | solution.py:730
  191.5 3.9 %collective-permute-done = f32[128,2048]{1,0:T(8,128)} collective-permute-done((f32[128,2048]{1,0:T(8,128)}, f32[128,2048]{1,0:T(8,128)}, u32[]{:S(2)}, u32[]{:S(2)}) %collective-permute-start) | collective-permute-done | bytes 1048608 | tf_op jit(solution)/shard_map/ppermute | solution.py:840
  195.4 0.0 copy-done.3
  195.4 2.2 add_convert_fusion
  197.6 0.0 collective-permute-done.2.far_partner
  197.6 0.0 collective-permute-done.3.far_both
  197.6 0.0 copy-done
  197.6 0.0 copy-done.1
  197.6 0.0 copy-done.2
  197.6 24.7 %table_grad.1 = f32[8000,2048]{1,0:T(8,128)} custom-call(s32[2048]{0:T(1024)S(1)} %bitcast.5, s32[128]{0:T(128)S(1)} %bitcast.6, bf16[2048,2048]{1,0:T(8,128)(2,1)} %get-tuple-element.22.dx_in, bf16[128,2048]{1,0:T(8,128)(2,1)S(1)} %copy-done, bf16[128,2048]{1,0:T(8,128)(2,1)S(1)} %collective-permute-done.1.far_across, ...), custom_call_target="tpu_custom_call" | custom-call | flops 26214400000 | bytes 65536000 | tf_op jit(solution)/shard_map/table_grad/pallas_call | solution.py:806
Async XLA Ops:
  158.6 15.1 %collective-permute-start.1 = (bf16[128,2048]{1,0:T(8,128)(2,1)}, bf16[128,2048]{1,0:T(8,128)(2,1)S(1)}, u32[]{:S(2)}, u32[]{:S(2)}) collective-permute-start(bf16[128,2048]{1,0:T(8,128)(2,1)} %get-tuple-element.23.far_own), channel_id=1, source_target_pairs={{0,2},{1,3},{2,0},{3,1},{4,6},{5,7},{6,4},{7,5},{8,10},{9,11},{10,... | collective-permute-start | bytes 1572872 | tf_op jit(solution)/shard_map/ppermute | solution.py:838
  158.9 38.7 %collective-permute-start.2 = (bf16[128,2048]{1,0:T(8,128)(2,1)}, bf16[128,2048]{1,0:T(8,128)(2,1)S(1)}, u32[]{:S(2)}, u32[]{:S(2)}) collective-permute-start(bf16[128,2048]{1,0:T(8,128)(2,1)} %get-tuple-element.23.far_own), channel_id=1, source_target_pairs={{0,1},{1,0},{2,3},{3,2},{4,5},{5,4},{6,7},{7,6},{8,9},{9,8},{10,11... | collective-permute-start | bytes 1572872 | tf_op jit(solution)/shard_map/ppermute | solution.py:839
  158.9 36.5 %collective-permute-start = (f32[128,2048]{1,0:T(8,128)}, f32[128,2048]{1,0:T(8,128)}, u32[]{:S(2)}, u32[]{:S(2)}) collective-permute-start(f32[128,2048]{1,0:T(8,128)} %get-tuple-element.19), channel_id=1, source_target_pairs={{0,2},{1,3},{2,0},{3,1},{4,6},{5,7},{6,4},{7,5},{8,10},{9,11},{10,... | collective-permute-start | bytes 3145736 | tf_op jit(solution)/shard_map/ppermute | solution.py:840
  173.7 23.9 %collective-permute-start.3 = (bf16[128,2048]{1,0:T(8,128)(2,1)S(1)}, bf16[128,2048]{1,0:T(8,128)(2,1)S(1)}, u32[]{:S(2)}, u32[]{:S(2)}) collective-permute-start(bf16[128,2048]{1,0:T(8,128)(2,1)S(1)} %collective-permute-done.1.far_across), channel_id=1, source_target_pairs={{0,1},{1,0},{2,3},{3,2},{4,5},{5,4},{6,7},{7,6},{8,9},{9,8},{10,11... | collective-permute-start | bytes 1572872 | tf_op jit(solution)/shard_map/ppermute | solution.py:842
  173.7 21.7 %copy-start.3 = (f32[128,2048]{1,0:T(8,128)S(1)}, f32[128,2048]{1,0:T(8,128)}, u32[]{:S(2)}) copy-start(f32[128,2048]{1,0:T(8,128)} %get-tuple-element.18) | copy-start | bytes 3145732
  173.7 23.9 %copy-start = (bf16[128,2048]{1,0:T(8,128)(2,1)S(1)}, bf16[128,2048]{1,0:T(8,128)(2,1)}, u32[]{:S(2)}) copy-start(bf16[128,2048]{1,0:T(8,128)(2,1)} %get-tuple-element.23.far_own) | copy-start | bytes 1572868
  173.7 23.9 %copy-start.1 = (s32[16,128]{1,0:T(8,128)S(1)}, s32[16,128]{1,0:T(8,128)}, u32[]{:S(2)}) copy-start(s32[16,128]{1,0:T(8,128)} %get-tuple-element.20) | copy-start | bytes 24580
  173.7 23.9 %copy-start.2 = (s32[1,128]{1,0:T(1,128)S(1)}, s32[1,128]{1,0:T(1,128)}, u32[]{:S(2)}) copy-start(s32[1,128]{1,0:T(1,128)} %get-tuple-element.21) | copy-start | bytes 1540

commit v5 on v4

--- a/solution.py
+++ b/solution.py
@@ -20,9 +20,9 @@
 PQ = 4
 
 R_IDS, R_DZ, R_DY, R_DC, R_NZ, R_NC, R_XZ, R_XY, R_XC = 0, 4, 8, 12, 16, 24, 28, 36, 44
-R_XM, R_X, R_NO, R_PC, R_PY, R_NY, N_R = 48, 52, 56, 60, 68, 72, 73
+R_XM, R_X, R_NO, R_PC, R_PY, R_NY, R_X2, N_R = 48, 52, 56, 60, 68, 72, 73, 74
 S_IDS, S_DZ, S_DY, S_DC, S_NZ, S_NC, S_XZ, S_XY, S_XC = 0, 3, 8, 12, 16, 26, 30, 40, 48
-S_XM, S_X, S_NO, S_PC, S_PY, S_NY, N_S = 52, 56, 60, 64, 72, 76, 77
+S_XM, S_X, S_NO, S_PC, S_PY, S_NY, S_X2, N_S = 52, 56, 60, 64, 72, 76, 77, 78
 L_W1, L_W2, L_XM, L_DX, L_YS, L_YB, L_DW, L_DO, L_K, N_L = 0, 1, 2, 3, 4, 5, 6, 8, 9, 13
 
 
@@ -420,8 +420,8 @@
 
     rows_loop(t, grad_x)
 
-    def dx_part(zz, yy, h):
-        return dx_o.at[pl.ds(pl.multiple_of(row(zz, c, yy) + h * th, th), th)]
+    def dx_part(zz, yy, h, cc=c):
+        return dx_o.at[pl.ds(pl.multiple_of(row(zz, cc, yy) + h * th, th), th)]
 
     def dx_own(h):
         return dxo.at[pl.ds(h * th, th)]
@@ -429,16 +429,32 @@
     def far_part(h):
         return far_o.at[pl.ds(h * th, th)]
 
+    def dx_at(k, h):
+        if k == 2:
+            return far_part(h)
+        return far_part(2) if k == 1 and h == 1 else dx_part(order[k], y, h)
+
     def dx_next(k, h):
-        here = dx_part(order[k], y, h)
-        return (here, here) if k == 1 else (here if k == 0 else far_part(h), far_part(h))
+        return dx_at(k, h), far_part(h) if k == 0 else dx_at(k, h)
 
     def dx_across(zz, src, h, act):
         act(remote(src, dx_part(zz, y, h), S_XY + 4 * h + zz, R_XY + 4 * h + zz, across))
 
     def dx_along(act):
         for h in range(2):
-            along(dx_own(h), dx_part(z, y, h), S_XZ + 5 * h, R_XZ + 4 * h, act)
+            for i, hop in enumerate((1, -1)):
+                to = z + hop
+                inside = middle & (to >= 1) & (to <= 2)
+
+                def go(dst, h=h, i=i, to=to):
+                    act(remote(dx_own(h), dst, S_XZ + 5 * h + i, R_XZ + 4 * h + z, {"data": to}))
+
+                there = (to >= 0) & (to <= 3)
+                if h == 0:
+                    pl.when(there)(lambda go=go: go(dx_part(z, y, 0)))
+                else:
+                    pl.when(there & jnp.logical_not(inside))(lambda go=go: go(dx_part(z, y, 1)))
+                    pl.when(inside)(lambda go=go: go(far_part(2)))
 
     def dx_pair(zz, act):
         act(remote(duo(dx_o, zz, c), duo(dx_o, zz, c), S_XC + zz, R_XC + zz, partner))
@@ -446,11 +462,15 @@
     def dx_got(k, on):
         zz = order[k]
         for h in range(2):
-            arrived(dx_part(zz, y, h) if k < 2 else far_part(h), R_XZ + 4 * h + zz)
+            arrived(dx_at(k, h), R_XZ + 4 * h + zz)
             if on:
                 pass_on(k, dx_next(k, h), S_XZ + 5 * h, R_XZ + 4 * h, start)
-            if k < 2:
+            if k + h < 2 and k < 2:
                 dx_across(zz, dx_part(zz, y, h), h, start)
+
+    def dx_first(zz, act):
+        for yy, s, q in ((y, S_XC + zz, R_XC + zz), (1 - y, S_X2, R_X2)):
+            act(remote(dx_part(zz, yy, 0), dx_part(zz, yy, 0), s, q, partner))
 
     def dx_hand(zz):
         for h in range(2):
@@ -461,12 +481,6 @@
         dx_across(z, dx_own(h), h, start)
     local(dxo, blk(dx_o, z, c, y), L_DX).start()
 
-    @pl.when(end)
-    def _():
-        d_got(2)
-
-    d_across(order[2], start)
-
     for q in range(PQ):
         part_pair(pd, rd, 0, q).wait_send()
 
@@ -475,6 +489,7 @@
     def _():
         n_far(0, True)
         n_far(1, True)
+        d_across(order[2], start)
 
     dx_along(start)
 
@@ -484,7 +499,13 @@
         n_pair(order[1], start)
 
     unit(1, pd)
-    pl.when(end)(lambda: n_far(0, False))
+
+    @pl.when(end)
+    def _():
+        n_far(0, False)
+        d_got(2)
+        d_across(order[2], start)
+
 
     @pl.when(middle)
     def _():
@@ -536,7 +557,8 @@
         rest[...] = lax.dot_general(hs[early_rows, n2 * tw :], d[early_rows, :], TN, preferred_element_type=F32)
         last = local(rest, dw2_o.at[pl.ds(n2 * tw, f % tw)], L_DW)
         last.start()
-    dx_hand(order[1])
+    arrived(dx_part(order[1], 1 - y, 0), R_XY + order[1])
+    dx_first(order[1], start)
     pl.when(end)(lambda: dx_got(2, False))
     if f % tw:
         last.wait()
@@ -556,8 +578,8 @@
     for b in range(2):
         n_along(b, sent)
         dx_across(z, dx_own(b), b, sent)
-        for k in range(2):
-            dx_across(order[k], dx_part(order[k], y, b), b, sent)
+        dx_across(order[b], dx_part(order[b], y, 0), 0, sent)
+    dx_across(order[0], dx_part(order[0], y, 1), 1, sent)
 
     @pl.when(middle)
     def _():
@@ -573,9 +595,12 @@
     n_cross(sent)
     for q in range(PQ):
         part_across(q).wait_send()
-    for zz in (z, *order[:2]):
+    for zz in (z, order[0]):
         arrived(duo(dx_o, zz, 1 - c), R_XC + zz)
         dx_pair(zz, sent)
+    arrived(dx_part(order[1], y, 0, 1 - c), R_XC + order[1])
+    arrived(dx_part(order[1], 1 - y, 0, 1 - c), R_X2)
+    dx_first(order[1], sent)
 
 
 def run_group(ids, xm, w1, w2, gain, d_out, shard_rows, tall):
@@ -590,7 +615,7 @@
         functools.partial(group_kernel, shard_rows, tall),
         out_shape=(
             sds((t, m), F32), sds((t, m), F32), sds((lines, LANES), I32), sds((1, LANES), I32), sds((16 * t, m), BF16),
-            sds((t, m), BF16), sds((m, f), F32), sds((f, m), F32),
+            sds((3 * t // 2, m), BF16), sds((m, f), F32), sds((f, m), F32),
             sds((4 * t, m), BF16), sds((4 * t, m), BF16), sds((4 * t, f), BF16), sds((4 * t, f), BF16),
         ),
         in_specs=[vmem, any_, any_, any_, vmem, any_],
@@ -755,14 +780,20 @@
     def far(cc, yy):
         return pl.multiple_of((1 - late) * (12 * t) + cc * (2 * t) + yy * t, t)
 
+    def second(cc, yy):
+        return pl.multiple_of((2 - late) * (4 * t) + cc * (2 * t) + yy * t + t // 2, t // 2)
+
     loop(0, 6, lambda k: near(k)[1].start())
-    for src, cc, yy in ((far_own, c, y), (far_across, c, 1 - y), (far_partner, 1 - c, y), (far_both, 1 - c, 1 - y)):
-        to = far(cc, yy)
-
-        def widen_far(i, src=src, to=to):
-            dxf[pl.ds(to + i, 16), :] = src[pl.ds(i, 16), :].astype(F32)
-
-        rows_loop(t, widen_far)
+    fars = ((far_own, c, y), (far_across, c, 1 - y), (far_partner, 1 - c, y), (far_both, 1 - c, 1 - y))
+
+    def widen_from(src, begin, to, rows):
+        def widen(i):
+            dxf[pl.ds(to + i, 16), :] = src[pl.ds(begin + i, 16), :].astype(F32)
+
+        rows_loop(rows, widen)
+
+    for src, cc, yy in fars:
+        widen_from(src, 0, far(cc, yy), t)
 
     def widen_piece(at, cp):
         cp.wait()
@@ -774,6 +805,8 @@
         rows_loop(at.size, widen)
 
     loop(0, 6, lambda k: widen_piece(*near(k)))
+    for src, cc, yy in fars:
+        widen_from(src, t, second(cc, yy), t // 2)
 
     def tile_out(i):
         slot = lax.rem(i, RING)

time: 223 us -> 227 us (1.018)
  waiting for transfers between devices: 16.9 us -> 22.6 us
    ppermute x1, waiting for transfers between devices: 13 us -> 18.6 us  [per_device(): far_x = lax.ppermute(far, 'tensor', over_y)]
where the time goes in v5:
time: 227 us; the launch traced here: 226 us
  Pallas kernels  198 us (87%)
  waiting for transfers between devices  22.6 us (10%)
  other arithmetic  2.45 us (1%)
    pallas_call x1, Pallas kernels, run_group(): pl.pallas_call(functools.partial(group_kernel, shard_rows, tall), out_sha...  146 us
    pallas_call x1, Pallas kernels, table_grad(): pl.pallas_call(functools.partial(table_kernel, tall), out_shape=jax.Shape...  24.9 us
    ppermute x1, waiting for transfers between devices, per_device(): far_x = lax.ppermute(far, 'tensor', over_y)  18.6 us
    pallas_call x1, Pallas kernels, finish_weights(): pl.pallas_call(weights_kernel, out_shape=(jax.ShapeDtypeStruct(p1.shape,...  17.8 us
    pallas_call x1, Pallas kernels, look_up(): pl.pallas_call(functools.partial(lookup_kernel, shard_rows), out_shape=ja...  9.84 us
  transfers between devices with their start and end apart: 4, of which 2 were waited for; matrix products, arithmetic and copies ran while one was open for 1% of the time, Pallas kernels for 8%

profile of v5, /device:TPU:0, one launch (start us, length us, event | category | flops | bytes accessed | tf_op | source)
XLA Modules:
  0.0 226.3 jit_solution(14968194172798017362)
XLA Ops:
  0.6 9.8 %look_up.1.xm_hbm = bf16[512,2048]{1,0:T(8,128)(2,1)} custom-call(s32[4,128]{1,0:T(4,128)} %bitcast.8, s32[4,128]{1,0:T(4,128)} %bitcast.9, bf16[1000,8,2048]{2,1,0:T(8,128)(2,1)} %bitcast.7), custom_call_target="tpu_custom_call" | custom-call | flops 16777216 | bytes 20971520 | tf_op jit(solution)/shard_map/look_up/pallas_call | solution.py:690
  10.5 145.9 %group_step.1 = (f32[128,2048]{1,0:T(8,128)}, f32[128,2048]{1,0:T(8,128)}, s32[16,128]{1,0:T(8,128)}, s32[1,128]{1,0:T(1,128)}, bf16[2048,2048]{1,0:T(8,128)(2,1...) custom-call(s32[4,128]{1,0:T(4,128)} %bitcast.10, ...), custom_call_target="tpu_custom_call" | custom-call | flops 53150220288 | bytes 268435456 | tf_op jit(solution)/shard_map/group_step/pallas_call | solution.py:614
  156.4 0.4 collective-permute-start.1
  156.8 0.0 collective-permute-start.2
  156.8 1.7 collective-permute-start
  158.5 18.6 %collective-permute-done.1.far_across = bf16[192,2048]{1,0:T(8,128)(2,1)S(1)} collective-permute-done((bf16[192,2048]{1,0:T(8,128)(2,1)}, bf16[192,2048]{1,0:T(8,128)(2,1)S(1)}, u32[]{:S(2)}, u32[]{:S(2)}) %collective-permute-start.1) | collective-permute-done | bytes 786464 | tf_op jit(solution)/shard_map/ppermute | solution.py:871
  177.1 0.0 collective-permute-start.3
  177.1 0.0 copy-start
  177.1 0.0 copy-start.1
  177.1 0.0 copy-start.2
  177.1 17.8 %finish_weights.1 = (f32[2048,1408]{1,0:T(8,128)}, f32[1408,2048]{1,0:T(8,128)}) custom-call(f32[2048,1408]{1,0:T(8,128)} %get-tuple-element.24.p1, f32[1408,2048]{1,0:T(8,128)} %get-tuple-element.25.p2, bf16[512,2048]{1,0:T(8,128)(2,1)} %get-tuple-element.26.nk_in, bf16[512,2048]{1,0:T(8,128)(2,1)} %get-tuple-element.27.dk_in, ...), custom_call_target="tpu_custom_call" | custom-call | flops 23068672000 | bytes 57671680 | tf_op jit(solution)/shard_map/finish_weights/pallas_call | solution.py:755
  194.8 4.0 %collective-permute-done = f32[128,2048]{1,0:T(8,128)} collective-permute-done((f32[128,2048]{1,0:T(8,128)}, f32[128,2048]{1,0:T(8,128)}, u32[]{:S(2)}, u32[]{:S(2)}) %collective-permute-start) | collective-permute-done | bytes 1048608 | tf_op jit(solution)/shard_map/ppermute | solution.py:873
  198.8 2.5 %add_convert_fusion = bf16[128,2048]{1,0:T(8,128)(2,1)} fusion(f32[128,2048]{1,0:T(8,128)} %get-tuple-element.18, f32[128,2048]{1,0:T(8,128)} %collective-permute-done), kind=kLoop, calls=%fused_computation | loop fusion | flops 524288 | bytes 2621440 | tf_op jit(solution)/shard_map/convert_element_type | solution.py:878
  201.3 0.0 collective-permute-done.2.far_partner
  201.3 0.0 collective-permute-done.3.far_both
  201.3 0.0 copy-done
  201.3 0.0 copy-done.1
  201.3 0.0 copy-done.2
  201.3 24.9 %table_grad.1 = f32[8000,2048]{1,0:T(8,128)} custom-call(s32[2048]{0:T(1024)S(1)} %bitcast.5, s32[128]{0:T(128)S(1)} %bitcast.6, bf16[2048,2048]{1,0:T(8,128)(2,1)} %get-tuple-element.22.dx_in, bf16[192,2048]{1,0:T(8,128)(2,1)S(1)} %copy-done, bf16[192,2048]{1,0:T(8,128)(2,1)S(1)} %collective-permute-done.1.far_across, ...), custom_call_target="tpu_custom_call" | custom-call | flops 26214400000 | bytes 65536000 | tf_op jit(solution)/shard_map/table_grad/pallas_call | solution.py:839
Async XLA Ops:
  156.4 20.7 %collective-permute-start.1 = (bf16[192,2048]{1,0:T(8,128)(2,1)}, bf16[192,2048]{1,0:T(8,128)(2,1)S(1)}, u32[]{:S(2)}, u32[]{:S(2)}) collective-permute-start(bf16[192,2048]{1,0:T(8,128)(2,1)} %get-tuple-element.23.far_own), channel_id=1, source_target_pairs={{0,2},{1,3},{2,0},{3,1},{4,6},{5,7},{6,4},{7,5},{8,10},{9,11},{10,... | collective-permute-start | bytes 2359304 | tf_op jit(solution)/shard_map/ppermute | solution.py:871
  156.8 44.5 %collective-permute-start.2 = (bf16[192,2048]{1,0:T(8,128)(2,1)}, bf16[192,2048]{1,0:T(8,128)(2,1)S(1)}, u32[]{:S(2)}, u32[]{:S(2)}) collective-permute-start(bf16[192,2048]{1,0:T(8,128)(2,1)} %get-tuple-element.23.far_own), channel_id=1, source_target_pairs={{0,1},{1,0},{2,3},{3,2},{4,5},{5,4},{6,7},{7,6},{8,9},{9,8},{10,11... | collective-permute-start | bytes 2359304 | tf_op jit(solution)/shard_map/ppermute | solution.py:872
  156.8 42.0 %collective-permute-start = (f32[128,2048]{1,0:T(8,128)}, f32[128,2048]{1,0:T(8,128)}, u32[]{:S(2)}, u32[]{:S(2)}) collective-permute-start(f32[128,2048]{1,0:T(8,128)} %get-tuple-element.19), channel_id=1, source_target_pairs={{0,2},{1,3},{2,0},{3,1},{4,6},{5,7},{6,4},{7,5},{8,10},{9,11},{10,... | collective-permute-start | bytes 3145736 | tf_op jit(solution)/shard_map/ppermute | solution.py:873
  177.1 24.2 %collective-permute-start.3 = (bf16[192,2048]{1,0:T(8,128)(2,1)S(1)}, bf16[192,2048]{1,0:T(8,128)(2,1)S(1)}, u32[]{:S(2)}, u32[]{:S(2)}) collective-permute-start(bf16[192,2048]{1,0:T(8,128)(2,1)S(1)} %collective-permute-done.1.far_across), channel_id=1, source_target_pairs={{0,1},{1,0},{2,3},{3,2},{4,5},{5,4},{6,7},{7,6},{8,9},{9,8},{10,11... | collective-permute-start | bytes 2359304 | tf_op jit(solution)/shard_map/ppermute | solution.py:875
  177.1 24.2 %copy-start = (bf16[192,2048]{1,0:T(8,128)(2,1)S(1)}, bf16[192,2048]{1,0:T(8,128)(2,1)}, u32[]{:S(2)}) copy-start(bf16[192,2048]{1,0:T(8,128)(2,1)} %get-tuple-element.23.far_own) | copy-start | bytes 2359300
  177.1 24.2 %copy-start.1 = (s32[16,128]{1,0:T(8,128)S(1)}, s32[16,128]{1,0:T(8,128)}, u32[]{:S(2)}) copy-start(s32[16,128]{1,0:T(8,128)} %get-tuple-element.20) | copy-start | bytes 24580
  177.1 24.2 %copy-start.2 = (s32[1,128]{1,0:T(1,128)S(1)}, s32[1,128]{1,0:T(1,128)}, u32[]{:S(2)}) copy-start(s32[1,128]{1,0:T(1,128)} %get-tuple-element.21) | copy-start | bytes 1540

commit v6 on v5

--- a/solution.py
+++ b/solution.py
@@ -382,12 +382,13 @@
         n_on(1, start)
         n_pair(order[1], start)
 
-    def unit(k, slopes):
+    def unit(k, slopes, between=lambda: None):
         zz = order[k]
         arrived(blk(d, zz, c, 1 - y), R_DY + zz)
         d_pair(zz, start)
         arrived(duo(n, zz, 1 - c), R_NC + zz)
         hidden(zz, slopes)
+        between()
         arrived(duo(d, zz, 1 - c), R_DC + zz)
         grad_hidden(zz, slopes)
 
@@ -459,9 +460,9 @@
     def dx_pair(zz, act):
         act(remote(duo(dx_o, zz, c), duo(dx_o, zz, c), S_XC + zz, R_XC + zz, partner))
 
-    def dx_got(k, on):
+    def dx_got(k, on, halves=(0, 1)):
         zz = order[k]
-        for h in range(2):
+        for h in halves:
             arrived(dx_at(k, h), R_XZ + 4 * h + zz)
             if on:
                 pass_on(k, dx_next(k, h), S_XZ + 5 * h, R_XZ + 4 * h, start)
@@ -523,43 +524,50 @@
         return here, local(here, dst.at[pl.ds(pl.multiple_of(i * tw, tw), tw)], L_DW + lax.rem(i, 2))
 
     def weight_tile(i, lhs, rhs, buf, dst):
-        pl.when(i >= 2)(lambda: flush(i - 2, buf, dst)[1].wait())
         here, out = flush(i, buf, dst)
         at = pl.ds(pl.multiple_of(i * tw, tw), tw)
         here[...] = lax.dot_general(lhs[early_rows, at], rhs[early_rows, :], TN, preferred_element_type=F32)
         out.start()
 
-    loop(0, n1 // 2, lambda i: weight_tile(i, n, dus, pf, dw1_o))
+    def dw1_tile(i):
+        pl.when(i >= 2)(lambda: flush(i - 2, pf, dw1_o)[1].wait())
+        weight_tile(i, n, dus, pf, dw1_o)
+
+    def dw2_tile(i):
+        pl.when(i < 2)(lambda: flush(n1 - 2 + i, pf, dw1_o)[1].wait())
+        pl.when(i >= 2)(lambda: flush(i - 2, pf, dw2_o)[1].wait())
+        weight_tile(i, hs, d, pf, dw2_o)
+
+    loop(0, n1 // 2, dw1_tile)
     pl.when(end)(lambda: n_far(1, False))
-    loop(n1 // 2, n1, lambda i: weight_tile(i, n, dus, pf, dw1_o))
-    for i in (n1 - 2, n1 - 1):
-        flush(i, pf, dw1_o)[1].wait()
-    pl.when(end)(lambda: dx_got(0, False))
+    loop(n1 // 2, n1, dw1_tile)
     n_far_pair()
     local(dxo, blk(dx_o, z, c, y), L_DX).wait()
     dx_hand(z)
+    loop(0, 2, dw2_tile)
+    pl.when(end)(lambda: dx_got(0, False))
     pl.when(middle)(lambda: dx_got(2, True))
-    unit(2, pd)
-    pl.when(end)(lambda: dx_got(1, False))
+    loop(2, n2 - 2, dw2_tile)
+    unit(2, pd, lambda: pl.when(end)(lambda: dx_got(1, False, (0,))))
+    pl.when(end)(lambda: dx_got(1, False, (1,)))
     kept = [
         local(src.at[late_rows], dst, L_K + i)
         for i, (src, dst) in enumerate(((n, nk_o), (d, dk_o), (hs, hk_o), (dus, duk_o)))
     ]
     for cp in kept:
         cp.start()
-    loop(0, n2 // 2, lambda i: weight_tile(i, hs, d, pd, dw2_o))
     dx_hand(order[0])
-    loop(n2 // 2, n2, lambda i: weight_tile(i, hs, d, pd, dw2_o))
-    for i in (n2 - 2, n2 - 1):
-        flush(i, pd, dw2_o)[1].wait()
+    loop(n2 - 2, n2, dw2_tile)
+    arrived(dx_part(order[1], 1 - y, 0), R_XY + order[1])
+    dx_first(order[1], start)
     if f % tw:
         rest = pd.at[pl.ds(0, f % tw)]
         rest[...] = lax.dot_general(hs[early_rows, n2 * tw :], d[early_rows, :], TN, preferred_element_type=F32)
-        last = local(rest, dw2_o.at[pl.ds(n2 * tw, f % tw)], L_DW)
+        last = local(rest, dw2_o.at[pl.ds(n2 * tw, f % tw)], L_DO)
         last.start()
-    arrived(dx_part(order[1], 1 - y, 0), R_XY + order[1])
-    dx_first(order[1], start)
     pl.when(end)(lambda: dx_got(2, False))
+    for i in (n2 - 2, n2 - 1):
+        flush(i, pf, dw2_o)[1].wait()
     if f % tw:
         last.wait()
     for cp in kept:

time: 227 us -> 222 us (0.978)
  Pallas kernels: 198 us -> 193 us
    pallas_call x1, Pallas kernels: 146 us -> 141 us  [run_group(): pl.pallas_call(functools.partial(group_kernel, shard_rows, tall), out_sha...]
where the time goes in v6:
time: 222 us; the launch traced here: 221 us
  Pallas kernels  193 us (87%)
  waiting for transfers between devices  22.7 us (10%)
  other arithmetic  2.45 us (1%)
    pallas_call x1, Pallas kernels, run_group(): pl.pallas_call(functools.partial(group_kernel, shard_rows, tall), out_sha...  141 us
    pallas_call x1, Pallas kernels, table_grad(): pl.pallas_call(functools.partial(table_kernel, tall), out_shape=jax.Shape...  24.9 us
    ppermute x1, waiting for transfers between devices, per_device(): far_x = lax.ppermute(far, 'tensor', over_y)  18.5 us
    pallas_call x1, Pallas kernels, finish_weights(): pl.pallas_call(weights_kernel, out_shape=(jax.ShapeDtypeStruct(p1.shape,...  17.8 us
    pallas_call x1, Pallas kernels, look_up(): pl.pallas_call(functools.partial(lookup_kernel, shard_rows), out_shape=ja...  9.84 us
  transfers between devices with their start and end apart: 4, of which 2 were waited for; matrix products, arithmetic and copies ran while one was open for 1% of the time, Pallas kernels for 8%

profile of v6, /device:TPU:0, one launch (start us, length us, event | category | flops | bytes accessed | tf_op | source)
XLA Modules:
  0.0 221.4 jit_solution(10059127261890043211)
XLA Ops:
  0.6 9.8 %look_up.1.xm_hbm = bf16[512,2048]{1,0:T(8,128)(2,1)} custom-call(s32[4,128]{1,0:T(4,128)} %bitcast.8, s32[4,128]{1,0:T(4,128)} %bitcast.9, bf16[1000,8,2048]{2,1,0:T(8,128)(2,1)} %bitcast.7), custom_call_target="tpu_custom_call" | custom-call | flops 16777216 | bytes 20971520 | tf_op jit(solution)/shard_map/look_up/pallas_call | solution.py:698
  10.5 140.7 %group_step.1 = (f32[128,2048]{1,0:T(8,128)}, f32[128,2048]{1,0:T(8,128)}, s32[16,128]{1,0:T(8,128)}, s32[1,128]{1,0:T(1,128)}, bf16[2048,2048]{1,0:T(8,128)(2,1...) custom-call(s32[4,128]{1,0:T(4,128)} %bitcast.10, ...), custom_call_target="tpu_custom_call" | custom-call | flops 53150220288 | bytes 268435456 | tf_op jit(solution)/shard_map/group_step/pallas_call | solution.py:622
  151.2 0.7 collective-permute-start.1
  151.9 0.0 collective-permute-start.2
  151.9 1.5 collective-permute-start
  153.4 18.5 %collective-permute-done.1.far_across = bf16[192,2048]{1,0:T(8,128)(2,1)S(1)} collective-permute-done((bf16[192,2048]{1,0:T(8,128)(2,1)}, bf16[192,2048]{1,0:T(8,128)(2,1)S(1)}, u32[]{:S(2)}, u32[]{:S(2)}) %collective-permute-start.1) | collective-permute-done | bytes 786464 | tf_op jit(solution)/shard_map/ppermute | solution.py:879
  171.9 0.0 collective-permute-start.3
  171.9 0.0 copy-start
  171.9 0.0 copy-start.1
  171.9 0.0 copy-start.2
  171.9 17.8 %finish_weights.1 = (f32[2048,1408]{1,0:T(8,128)}, f32[1408,2048]{1,0:T(8,128)}) custom-call(f32[2048,1408]{1,0:T(8,128)} %get-tuple-element.24.p1, f32[1408,2048]{1,0:T(8,128)} %get-tuple-element.25.p2, bf16[512,2048]{1,0:T(8,128)(2,1)} %get-tuple-element.26.nk_in, bf16[512,2048]{1,0:T(8,128)(2,1)} %get-tuple-element.27.dk_in, ...), custom_call_target="tpu_custom_call" | custom-call | flops 23068672000 | bytes 57671680 | tf_op jit(solution)/shard_map/finish_weights/pallas_call | solution.py:763
  189.7 4.2 %collective-permute-done = f32[128,2048]{1,0:T(8,128)} collective-permute-done((f32[128,2048]{1,0:T(8,128)}, f32[128,2048]{1,0:T(8,128)}, u32[]{:S(2)}, u32[]{:S(2)}) %collective-permute-start) | collective-permute-done | bytes 1048608 | tf_op jit(solution)/shard_map/ppermute | solution.py:881
  193.9 2.5 %add_convert_fusion = bf16[128,2048]{1,0:T(8,128)(2,1)} fusion(f32[128,2048]{1,0:T(8,128)} %get-tuple-element.18, f32[128,2048]{1,0:T(8,128)} %collective-permute-done), kind=kLoop, calls=%fused_computation | loop fusion | flops 524288 | bytes 2621440 | tf_op jit(solution)/shard_map/convert_element_type | solution.py:886
  196.3 0.0 collective-permute-done.2.far_partner
  196.3 0.0 collective-permute-done.3.far_both
  196.4 0.0 copy-done
  196.4 0.0 copy-done.1
  196.4 0.0 copy-done.2
  196.4 24.9 %table_grad.1 = f32[8000,2048]{1,0:T(8,128)} custom-call(s32[2048]{0:T(1024)S(1)} %bitcast.5, s32[128]{0:T(128)S(1)} %bitcast.6, bf16[2048,2048]{1,0:T(8,128)(2,1)} %get-tuple-element.22.dx_in, bf16[192,2048]{1,0:T(8,128)(2,1)S(1)} %copy-done, bf16[192,2048]{1,0:T(8,128)(2,1)S(1)} %collective-permute-done.1.far_across, ...), custom_call_target="tpu_custom_call" | custom-call | flops 26214400000 | bytes 65536000 | tf_op jit(solution)/shard_map/table_grad/pallas_call | solution.py:847
Async XLA Ops:
  151.2 20.7 %collective-permute-start.1 = (bf16[192,2048]{1,0:T(8,128)(2,1)}, bf16[192,2048]{1,0:T(8,128)(2,1)S(1)}, u32[]{:S(2)}, u32[]{:S(2)}) collective-permute-start(bf16[192,2048]{1,0:T(8,128)(2,1)} %get-tuple-element.23.far_own), channel_id=1, source_target_pairs={{0,2},{1,3},{2,0},{3,1},{4,6},{5,7},{6,4},{7,5},{8,10},{9,11},{10,... | collective-permute-start | bytes 2359304 | tf_op jit(solution)/shard_map/ppermute | solution.py:879
  151.9 44.4 %collective-permute-start.2 = (bf16[192,2048]{1,0:T(8,128)(2,1)}, bf16[192,2048]{1,0:T(8,128)(2,1)S(1)}, u32[]{:S(2)}, u32[]{:S(2)}) collective-permute-start(bf16[192,2048]{1,0:T(8,128)(2,1)} %get-tuple-element.23.far_own), channel_id=1, source_target_pairs={{0,1},{1,0},{2,3},{3,2},{4,5},{5,4},{6,7},{7,6},{8,9},{9,8},{10,11... | collective-permute-start | bytes 2359304 | tf_op jit(solution)/shard_map/ppermute | solution.py:880
  151.9 42.0 %collective-permute-start = (f32[128,2048]{1,0:T(8,128)}, f32[128,2048]{1,0:T(8,128)}, u32[]{:S(2)}, u32[]{:S(2)}) collective-permute-start(f32[128,2048]{1,0:T(8,128)} %get-tuple-element.19), channel_id=1, source_target_pairs={{0,2},{1,3},{2,0},{3,1},{4,6},{5,7},{6,4},{7,5},{8,10},{9,11},{10,... | collective-permute-start | bytes 3145736 | tf_op jit(solution)/shard_map/ppermute | solution.py:881
  171.9 24.4 %collective-permute-start.3 = (bf16[192,2048]{1,0:T(8,128)(2,1)S(1)}, bf16[192,2048]{1,0:T(8,128)(2,1)S(1)}, u32[]{:S(2)}, u32[]{:S(2)}) collective-permute-start(bf16[192,2048]{1,0:T(8,128)(2,1)S(1)} %collective-permute-done.1.far_across), channel_id=1, source_target_pairs={{0,1},{1,0},{2,3},{3,2},{4,5},{5,4},{6,7},{7,6},{8,9},{9,8},{10,11... | collective-permute-start | bytes 2359304 | tf_op jit(solution)/shard_map/ppermute | solution.py:883
  171.9 24.4 %copy-start = (bf16[192,2048]{1,0:T(8,128)(2,1)S(1)}, bf16[192,2048]{1,0:T(8,128)(2,1)}, u32[]{:S(2)}) copy-start(bf16[192,2048]{1,0:T(8,128)(2,1)} %get-tuple-element.23.far_own) | copy-start | bytes 2359300
  171.9 24.4 %copy-start.1 = (s32[16,128]{1,0:T(8,128)S(1)}, s32[16,128]{1,0:T(8,128)}, u32[]{:S(2)}) copy-start(s32[16,128]{1,0:T(8,128)} %get-tuple-element.20) | copy-start | bytes 24580
  171.9 24.4 %copy-start.2 = (s32[1,128]{1,0:T(1,128)S(1)}, s32[1,128]{1,0:T(1,128)}, u32[]{:S(2)}) copy-start(s32[1,128]{1,0:T(1,128)} %get-tuple-element.21) | copy-start | bytes 1540

commit v7 on v6

--- a/solution.py
+++ b/solution.py
@@ -349,12 +349,12 @@
     for q in range(PQ):
         part_pair(pf, rf, 1, q).wait_send()
 
-    th = t // 2
+    th, tz = t // 2, t // 4
 
     def n_parts(k, lands):
         own, other = blk(n, order[k], c, y), blk(n, order[k], c, 1 - y)
         if lands == 2:
-            other = other.at[pl.ds(0, th)]
+            other = other.at[pl.ds(0, tz)]
         return (own, y), (other, 1 - y)
 
     def n_got(k):
@@ -366,8 +366,8 @@
             pass_on(k, ref, S_NZ + 5 * b, R_NZ + 4 * b, act)
 
     def n_cross(act):
-        half_own = blk(n, order[2], c, y).at[pl.ds(th, th)]
-        act(remote(half_own, half_own, S_NY, R_NY, across))
+        most = blk(n, order[2], c, y).at[pl.ds(tz, t - tz)]
+        act(remote(most, most, S_NY, R_NY, across))
 
     def n_pair(zz, act):
         act(remote(duo(n, zz, c), duo(n, zz, c), S_NC + zz, R_NC + zz, partner))
@@ -384,10 +384,17 @@
 
     def unit(k, slopes, between=lambda: None):
         zz = order[k]
-        arrived(blk(d, zz, c, 1 - y), R_DY + zz)
-        d_pair(zz, start)
+
+        def pair():
+            arrived(blk(d, zz, c, 1 - y), R_DY + zz)
+            d_pair(zz, start)
+
+        if k < 2:
+            pair()
         arrived(duo(n, zz, 1 - c), R_NC + zz)
         hidden(zz, slopes)
+        if k == 2:
+            pair()
         between()
         arrived(duo(d, zz, 1 - c), R_DC + zz)
         grad_hidden(zz, slopes)
@@ -401,7 +408,7 @@
             n_cross(start)
 
     def n_far_pair():
-        arrived(blk(n, order[2], c, 1 - y).at[pl.ds(th, th)], R_NY)
+        arrived(blk(n, order[2], c, 1 - y).at[pl.ds(tz, t - tz)], R_NY)
         n_pair(order[2], start)
 
     unit(0, pf)
@@ -648,23 +655,18 @@
     total, m = out_hbm.shape
     t = total // 4
     per = 32
-    chunks = total // per
     r = lax.axis_index("tensor")
     spread = (1 << (shard_rows.bit_length() - 1)) - 1
 
-    def fetch(k):
-        def some(j, carry):
-            for u in range(8):
-                p = k * per + j * 8 + u
-                row = ids_smem[jnp.right_shift(p, 7), p & (LANES - 1)]
-                near = row - r * shard_rows
-                near = jnp.where((near >= 0) & (near < shard_rows), near, row & spread)
-                pltpu.make_async_copy(table.at[jnp.right_shift(near, 3)], got.at[p], sem.at[k]).start()
-            return carry
-
-        lax.fori_loop(0, per // 8, some, 0)
-
-    loop(0, chunks, fetch)
+    def fetch(b):
+        for u in range(LANES):
+            row = ids_smem[b, u]
+            near = row - r * shard_rows
+            near = jnp.where((near >= 0) & (near < shard_rows), near, row & spread)
+            to = got.at[b * LANES + u]
+            pltpu.make_async_copy(table.at[jnp.right_shift(near, 3)], to, sem.at[b * (LANES // per) + u // per]).start()
+
+    loop(0, total // LANES, fetch)
     spot = lax.broadcasted_iota(I32, (per, 8 * per), 1)
     token = lax.broadcasted_iota(I32, (per, 8 * per), 0)
     same = lax.broadcasted_iota(I32, (LANES, LANES), 0) == lax.broadcasted_iota(I32, (LANES, LANES), 1)

time: 222 us -> 224 us (level)
  Pallas kernels: 193 us -> 196 us
    pallas_call x1, Pallas kernels: 141 us -> 143 us  [run_group(): pl.pallas_call(functools.partial(group_kernel, shard_rows, tall), out_sha...]
where the time goes in v7:
time: 224 us
  Pallas kernels  196 us (88%)
  waiting for transfers between devices  22.7 us (10%)
  other arithmetic  2.45 us (1%)
    pallas_call x1, Pallas kernels, run_group(): pl.pallas_call(functools.partial(group_kernel, shard_rows, tall), out_sha...  143 us
    pallas_call x1, Pallas kernels, table_grad(): pl.pallas_call(functools.partial(table_kernel, tall), out_shape=jax.Shape...  24.9 us
    ppermute x1, waiting for transfers between devices, per_device(): far_x = lax.ppermute(far, 'tensor', over_y)  18.5 us
    pallas_call x1, Pallas kernels, finish_weights(): pl.pallas_call(weights_kernel, out_shape=(jax.ShapeDtypeStruct(p1.shape,...  17.8 us
    pallas_call x1, Pallas kernels, look_up(): pl.pallas_call(functools.partial(lookup_kernel, shard_rows), out_shape=ja...  9.86 us
  transfers between devices with their start and end apart: 4, of which 2 were waited for; matrix products, arithmetic and copies ran while one was open for 1% of the time, Pallas kernels for 8%

profile of v7, /device:TPU:0, one launch (start us, length us, event | category | flops | bytes accessed | tf_op | source)
XLA Modules:
  0.0 224.2 jit_solution(11792796226616102990)
XLA Ops:
  0.6 9.9 %look_up.1.xm_hbm = bf16[512,2048]{1,0:T(8,128)(2,1)} custom-call(s32[4,128]{1,0:T(4,128)} %bitcast.8, s32[4,128]{1,0:T(4,128)} %bitcast.9, bf16[1000,8,2048]{2,1,0:T(8,128)(2,1)} %bitcast.7), custom_call_target="tpu_custom_call" | custom-call | flops 16777216 | bytes 20971520 | tf_op jit(solution)/shard_map/look_up/pallas_call | solution.py:700
  10.5 143.5 %group_step.1 = (f32[128,2048]{1,0:T(8,128)}, f32[128,2048]{1,0:T(8,128)}, s32[16,128]{1,0:T(8,128)}, s32[1,128]{1,0:T(1,128)}, bf16[2048,2048]{1,0:T(8,128)(2,1...) custom-call(s32[4,128]{1,0:T(4,128)} %bitcast.10, ...), custom_call_target="tpu_custom_call" | custom-call | flops 53150220288 | bytes 268435456 | tf_op jit(solution)/shard_map/group_step/pallas_call | solution.py:629
  154.0 0.2 collective-permute-start.1
  154.2 0.3 collective-permute-start.2
  154.5 1.7 collective-permute-start
  156.2 18.5 %collective-permute-done.1.far_across = bf16[192,2048]{1,0:T(8,128)(2,1)S(1)} collective-permute-done((bf16[192,2048]{1,0:T(8,128)(2,1)}, bf16[192,2048]{1,0:T(8,128)(2,1)S(1)}, u32[]{:S(2)}, u32[]{:S(2)}) %collective-permute-start.1) | collective-permute-done | bytes 786464 | tf_op jit(solution)/shard_map/ppermute | solution.py:881
  174.7 0.0 collective-permute-start.3
  174.7 0.0 copy-start
  174.7 0.0 copy-start.1
  174.7 0.0 copy-start.2
  174.7 17.8 %finish_weights.1 = (f32[2048,1408]{1,0:T(8,128)}, f32[1408,2048]{1,0:T(8,128)}) custom-call(f32[2048,1408]{1,0:T(8,128)} %get-tuple-element.24.p1, f32[1408,2048]{1,0:T(8,128)} %get-tuple-element.25.p2, bf16[512,2048]{1,0:T(8,128)(2,1)} %get-tuple-element.26.nk_in, bf16[512,2048]{1,0:T(8,128)(2,1)} %get-tuple-element.27.dk_in, ...), custom_call_target="tpu_custom_call" | custom-call | flops 23068672000 | bytes 57671680 | tf_op jit(solution)/shard_map/finish_weights/pallas_call | solution.py:765
  192.5 4.2 %collective-permute-done = f32[128,2048]{1,0:T(8,128)} collective-permute-done((f32[128,2048]{1,0:T(8,128)}, f32[128,2048]{1,0:T(8,128)}, u32[]{:S(2)}, u32[]{:S(2)}) %collective-permute-start) | collective-permute-done | bytes 1048608 | tf_op jit(solution)/shard_map/ppermute | solution.py:883
  196.7 2.5 %add_convert_fusion = bf16[128,2048]{1,0:T(8,128)(2,1)} fusion(f32[128,2048]{1,0:T(8,128)} %get-tuple-element.18, f32[128,2048]{1,0:T(8,128)} %collective-permute-done), kind=kLoop, calls=%fused_computation | loop fusion | flops 524288 | bytes 2621440 | tf_op jit(solution)/shard_map/convert_element_type | solution.py:888
  199.1 0.0 collective-permute-done.2.far_partner
  199.1 0.0 collective-permute-done.3.far_both
  199.1 0.0 copy-done
  199.1 0.0 copy-done.1
  199.1 0.0 copy-done.2
  199.1 24.9 %table_grad.1 = f32[8000,2048]{1,0:T(8,128)} custom-call(s32[2048]{0:T(1024)S(1)} %bitcast.5, s32[128]{0:T(128)S(1)} %bitcast.6, bf16[2048,2048]{1,0:T(8,128)(2,1)} %get-tuple-element.22.dx_in, bf16[192,2048]{1,0:T(8,128)(2,1)S(1)} %copy-done, bf16[192,2048]{1,0:T(8,128)(2,1)S(1)} %collective-permute-done.1.far_across, ...), custom_call_target="tpu_custom_call" | custom-call | flops 26214400000 | bytes 65536000 | tf_op jit(solution)/shard_map/table_grad/pallas_call | solution.py:849
Async XLA Ops:
  154.0 20.7 %collective-permute-start.1 = (bf16[192,2048]{1,0:T(8,128)(2,1)}, bf16[192,2048]{1,0:T(8,128)(2,1)S(1)}, u32[]{:S(2)}, u32[]{:S(2)}) collective-permute-start(bf16[192,2048]{1,0:T(8,128)(2,1)} %get-tuple-element.23.far_own), channel_id=1, source_target_pairs={{0,2},{1,3},{2,0},{3,1},{4,6},{5,7},{6,4},{7,5},{8,10},{9,11},{10,... | collective-permute-start | bytes 2359304 | tf_op jit(solution)/shard_map/ppermute | solution.py:881
  154.2 44.9 %collective-permute-start.2 = (bf16[192,2048]{1,0:T(8,128)(2,1)}, bf16[192,2048]{1,0:T(8,128)(2,1)S(1)}, u32[]{:S(2)}, u32[]{:S(2)}) collective-permute-start(bf16[192,2048]{1,0:T(8,128)(2,1)} %get-tuple-element.23.far_own), channel_id=1, source_target_pairs={{0,1},{1,0},{2,3},{3,2},{4,5},{5,4},{6,7},{7,6},{8,9},{9,8},{10,11... | collective-permute-start | bytes 2359304 | tf_op jit(solution)/shard_map/ppermute | solution.py:882
  154.5 42.2 %collective-permute-start = (f32[128,2048]{1,0:T(8,128)}, f32[128,2048]{1,0:T(8,128)}, u32[]{:S(2)}, u32[]{:S(2)}) collective-permute-start(f32[128,2048]{1,0:T(8,128)} %get-tuple-element.19), channel_id=1, source_target_pairs={{0,2},{1,3},{2,0},{3,1},{4,6},{5,7},{6,4},{7,5},{8,10},{9,11},{10,... | collective-permute-start | bytes 3145736 | tf_op jit(solution)/shard_map/ppermute | solution.py:883
  174.7 24.4 %collective-permute-start.3 = (bf16[192,2048]{1,0:T(8,128)(2,1)S(1)}, bf16[192,2048]{1,0:T(8,128)(2,1)S(1)}, u32[]{:S(2)}, u32[]{:S(2)}) collective-permute-start(bf16[192,2048]{1,0:T(8,128)(2,1)S(1)} %collective-permute-done.1.far_across), channel_id=1, source_target_pairs={{0,1},{1,0},{2,3},{3,2},{4,5},{5,4},{6,7},{7,6},{8,9},{9,8},{10,11... | collective-permute-start | bytes 2359304 | tf_op jit(solution)/shard_map/ppermute | solution.py:885
  174.7 24.4 %copy-start = (bf16[192,2048]{1,0:T(8,128)(2,1)S(1)}, bf16[192,2048]{1,0:T(8,128)(2,1)}, u32[]{:S(2)}) copy-start(bf16[192,2048]{1,0:T(8,128)(2,1)} %get-tuple-element.23.far_own) | copy-start | bytes 2359300
  174.7 24.4 %copy-start.1 = (s32[16,128]{1,0:T(8,128)S(1)}, s32[16,128]{1,0:T(8,128)}, u32[]{:S(2)}) copy-start(s32[16,128]{1,0:T(8,128)} %get-tuple-element.20) | copy-start | bytes 24580
  174.7 24.4 %copy-start.2 = (s32[1,128]{1,0:T(1,128)S(1)}, s32[1,128]{1,0:T(1,128)}, u32[]{:S(2)}) copy-start(s32[1,128]{1,0:T(1,128)} %get-tuple-element.21) | copy-start | bytes 1540

commit v8 on v6

--- a/solution.py
+++ b/solution.py
@@ -266,10 +266,10 @@
             to = pl.ds(off, w)
             u = jnp.dot(n[at, :], w1[:, to], preferred_element_type=F32).astype(BF16).astype(F32)
             uu = u * u
-            th = jnp.tanh(GELU_A * (u + GELU_B * (uu * u)))
-            cdf = 0.5 * (1.0 + th)
+            half_th = 0.5 * jnp.tanh(u * (GELU_A + (GELU_A * GELU_B) * uu))
+            cdf = 0.5 + half_th
             hs[at, to] = (u * cdf).astype(BF16)
-            slopes[:, to] = cdf + (0.5 * GELU_A) * u * (1.0 - th * th) * (1.0 + (3.0 * GELU_B) * uu)
+            slopes[:, to] = cdf + (u * (cdf * (0.5 - half_th))) * (2.0 * GELU_A + (6.0 * GELU_A * GELU_B) * uu)
 
         tiles(f, 256, body)
 
@@ -349,12 +349,12 @@
     for q in range(PQ):
         part_pair(pf, rf, 1, q).wait_send()
 
-    th = t // 2
+    th, tz = t // 2, 3 * t // 4
 
     def n_parts(k, lands):
         own, other = blk(n, order[k], c, y), blk(n, order[k], c, 1 - y)
         if lands == 2:
-            other = other.at[pl.ds(0, th)]
+            other = other.at[pl.ds(0, tz)]
         return (own, y), (other, 1 - y)
 
     def n_got(k):
@@ -366,8 +366,8 @@
             pass_on(k, ref, S_NZ + 5 * b, R_NZ + 4 * b, act)
 
     def n_cross(act):
-        half_own = blk(n, order[2], c, y).at[pl.ds(th, th)]
-        act(remote(half_own, half_own, S_NY, R_NY, across))
+        most = blk(n, order[2], c, y).at[pl.ds(tz, t - tz)]
+        act(remote(most, most, S_NY, R_NY, across))
 
     def n_pair(zz, act):
         act(remote(duo(n, zz, c), duo(n, zz, c), S_NC + zz, R_NC + zz, partner))
@@ -401,7 +401,7 @@
             n_cross(start)
 
     def n_far_pair():
-        arrived(blk(n, order[2], c, 1 - y).at[pl.ds(th, th)], R_NY)
+        arrived(blk(n, order[2], c, 1 - y).at[pl.ds(tz, t - tz)], R_NY)
         n_pair(order[2], start)
 
     unit(0, pf)

time: 222 us -> 222 us (level)
  no operation moved by 1% of the time
where the time goes in v8:
time: 222 us
  Pallas kernels  195 us (88%)
  waiting for transfers between devices  21.5 us (10%)
  other arithmetic  2.45 us (1%)
    pallas_call x1, Pallas kernels, run_group(): pl.pallas_call(functools.partial(group_kernel, shard_rows, tall), out_sha...  142 us
    pallas_call x1, Pallas kernels, table_grad(): pl.pallas_call(functools.partial(table_kernel, tall), out_shape=jax.Shape...  24.9 us
    ppermute x1, waiting for transfers between devices, per_device(): far_x = lax.ppermute(far, 'tensor', over_y)  18.6 us
    pallas_call x1, Pallas kernels, finish_weights(): pl.pallas_call(weights_kernel, out_shape=(jax.ShapeDtypeStruct(p1.shape,...  17.8 us
    pallas_call x1, Pallas kernels, look_up(): pl.pallas_call(functools.partial(lookup_kernel, shard_rows), out_shape=ja...  9.84 us
  transfers between devices with their start and end apart: 4, of which 2 were waited for; matrix products, arithmetic and copies ran while one was open for 1% of the time, Pallas kernels for 8%

profile of v8, /device:TPU:0, one launch (start us, length us, event | category | flops | bytes accessed | tf_op | source)
XLA Modules:
  0.0 221.8 jit_solution(17178635035021198924)
XLA Ops:
  0.6 9.8 %look_up.1.xm_hbm = bf16[512,2048]{1,0:T(8,128)(2,1)} custom-call(s32[4,128]{1,0:T(4,128)} %bitcast.8, s32[4,128]{1,0:T(4,128)} %bitcast.9, bf16[1000,8,2048]{2,1,0:T(8,128)(2,1)} %bitcast.7), custom_call_target="tpu_custom_call" | custom-call | flops 16777216 | bytes 20971520 | tf_op jit(solution)/shard_map/look_up/pallas_call | solution.py:698
  10.5 142.5 %group_step.1 = (f32[128,2048]{1,0:T(8,128)}, f32[128,2048]{1,0:T(8,128)}, s32[16,128]{1,0:T(8,128)}, s32[1,128]{1,0:T(1,128)}, bf16[2048,2048]{1,0:T(8,128)(2,1...) custom-call(s32[4,128]{1,0:T(4,128)} %bitcast.10, ...), custom_call_target="tpu_custom_call" | custom-call | flops 53150220288 | bytes 268435456 | tf_op jit(solution)/shard_map/group_step/pallas_call | solution.py:622
  153.0 1.8 collective-permute-start.1
  154.7 0.0 collective-permute-start.2
  154.7 0.3 collective-permute-start
  155.1 18.6 %collective-permute-done.1.far_across = bf16[192,2048]{1,0:T(8,128)(2,1)S(1)} collective-permute-done((bf16[192,2048]{1,0:T(8,128)(2,1)}, bf16[192,2048]{1,0:T(8,128)(2,1)S(1)}, u32[]{:S(2)}, u32[]{:S(2)}) %collective-permute-start.1) | collective-permute-done | bytes 786464 | tf_op jit(solution)/shard_map/ppermute | solution.py:879
  173.6 0.0 collective-permute-start.3
  173.7 0.0 copy-start
  173.7 0.0 copy-start.1
  173.7 0.0 copy-start.2
  173.7 17.8 %finish_weights.1 = (f32[2048,1408]{1,0:T(8,128)}, f32[1408,2048]{1,0:T(8,128)}) custom-call(f32[2048,1408]{1,0:T(8,128)} %get-tuple-element.24.p1, f32[1408,2048]{1,0:T(8,128)} %get-tuple-element.25.p2, bf16[512,2048]{1,0:T(8,128)(2,1)} %get-tuple-element.26.nk_in, bf16[512,2048]{1,0:T(8,128)(2,1)} %get-tuple-element.27.dk_in, ...), custom_call_target="tpu_custom_call" | custom-call | flops 23068672000 | bytes 57671680 | tf_op jit(solution)/shard_map/finish_weights/pallas_call | solution.py:763
  191.4 2.9 %collective-permute-done = f32[128,2048]{1,0:T(8,128)} collective-permute-done((f32[128,2048]{1,0:T(8,128)}, f32[128,2048]{1,0:T(8,128)}, u32[]{:S(2)}, u32[]{:S(2)}) %collective-permute-start) | collective-permute-done | bytes 1048608 | tf_op jit(solution)/shard_map/ppermute | solution.py:881
  194.3 2.5 %add_convert_fusion = bf16[128,2048]{1,0:T(8,128)(2,1)} fusion(f32[128,2048]{1,0:T(8,128)} %get-tuple-element.18, f32[128,2048]{1,0:T(8,128)} %collective-permute-done), kind=kLoop, calls=%fused_computation | loop fusion | flops 524288 | bytes 2621440 | tf_op jit(solution)/shard_map/convert_element_type | solution.py:886
  196.7 0.0 collective-permute-done.2.far_partner
  196.8 0.0 collective-permute-done.3.far_both
  196.8 0.0 copy-done
  196.8 0.0 copy-done.1
  196.8 0.0 copy-done.2
  196.8 24.9 %table_grad.1 = f32[8000,2048]{1,0:T(8,128)} custom-call(s32[2048]{0:T(1024)S(1)} %bitcast.5, s32[128]{0:T(128)S(1)} %bitcast.6, bf16[2048,2048]{1,0:T(8,128)(2,1)} %get-tuple-element.22.dx_in, bf16[192,2048]{1,0:T(8,128)(2,1)S(1)} %copy-done, bf16[192,2048]{1,0:T(8,128)(2,1)S(1)} %collective-permute-done.1.far_across, ...), custom_call_target="tpu_custom_call" | custom-call | flops 26214400000 | bytes 65536000 | tf_op jit(solution)/shard_map/table_grad/pallas_call | solution.py:847
Async XLA Ops:
  153.0 20.7 %collective-permute-start.1 = (bf16[192,2048]{1,0:T(8,128)(2,1)}, bf16[192,2048]{1,0:T(8,128)(2,1)S(1)}, u32[]{:S(2)}, u32[]{:S(2)}) collective-permute-start(bf16[192,2048]{1,0:T(8,128)(2,1)} %get-tuple-element.23.far_own), channel_id=1, source_target_pairs={{0,2},{1,3},{2,0},{3,1},{4,6},{5,7},{6,4},{7,5},{8,10},{9,11},{10,... | collective-permute-start | bytes 2359304 | tf_op jit(solution)/shard_map/ppermute | solution.py:879
  154.7 42.0 %collective-permute-start.2 = (bf16[192,2048]{1,0:T(8,128)(2,1)}, bf16[192,2048]{1,0:T(8,128)(2,1)S(1)}, u32[]{:S(2)}, u32[]{:S(2)}) collective-permute-start(bf16[192,2048]{1,0:T(8,128)(2,1)} %get-tuple-element.23.far_own), channel_id=1, source_target_pairs={{0,1},{1,0},{2,3},{3,2},{4,5},{5,4},{6,7},{7,6},{8,9},{9,8},{10,11... | collective-permute-start | bytes 2359304 | tf_op jit(solution)/shard_map/ppermute | solution.py:880
  154.7 39.6 %collective-permute-start = (f32[128,2048]{1,0:T(8,128)}, f32[128,2048]{1,0:T(8,128)}, u32[]{:S(2)}, u32[]{:S(2)}) collective-permute-start(f32[128,2048]{1,0:T(8,128)} %get-tuple-element.19), channel_id=1, source_target_pairs={{0,2},{1,3},{2,0},{3,1},{4,6},{5,7},{6,4},{7,5},{8,10},{9,11},{10,... | collective-permute-start | bytes 3145736 | tf_op jit(solution)/shard_map/ppermute | solution.py:881
  173.6 23.1 %collective-permute-start.3 = (bf16[192,2048]{1,0:T(8,128)(2,1)S(1)}, bf16[192,2048]{1,0:T(8,128)(2,1)S(1)}, u32[]{:S(2)}, u32[]{:S(2)}) collective-permute-start(bf16[192,2048]{1,0:T(8,128)(2,1)S(1)} %collective-permute-done.1.far_across), channel_id=1, source_target_pairs={{0,1},{1,0},{2,3},{3,2},{4,5},{5,4},{6,7},{7,6},{8,9},{9,8},{10,11... | collective-permute-start | bytes 2359304 | tf_op jit(solution)/shard_map/ppermute | solution.py:883
  173.7 23.1 %copy-start = (bf16[192,2048]{1,0:T(8,128)(2,1)S(1)}, bf16[192,2048]{1,0:T(8,128)(2,1)}, u32[]{:S(2)}) copy-start(bf16[192,2048]{1,0:T(8,128)(2,1)} %get-tuple-element.23.far_own) | copy-start | bytes 2359300
  173.7 23.1 %copy-start.1 = (s32[16,128]{1,0:T(8,128)S(1)}, s32[16,128]{1,0:T(8,128)}, u32[]{:S(2)}) copy-start(s32[16,128]{1,0:T(8,128)} %get-tuple-element.20) | copy-start | bytes 24580
  173.7 23.1 %copy-start.2 = (s32[1,128]{1,0:T(1,128)S(1)}, s32[1,128]{1,0:T(1,128)}, u32[]{:S(2)}) copy-start(s32[1,128]{1,0:T(1,128)} %get-tuple-element.21) | copy-start | bytes 1540
